TPU v7x, 128 devices: a whole 4x4x4 slice. The times are simulated.
128 devices in a mesh: row: 32 (over x, z, core), col: 4 (over y).
Axes of the slice: x: 4, y: 4, z: 4, core: 2. Of those that a mesh axis runs over, the one named last changes fastest.
Arguments:
- eigvecs: bfloat16 [49152, 4096], P('row', 'col'), may hold values from -41 to 41
- reflectors: bfloat16 [8, 49152, 128], P(None, 'row'), as said below
- factors: float32 [8, 128, 128], replicated, as said below
Outputs:
- vectors: bfloat16 [49152, 4096], P('row', 'col')
- deviation: float32 [4096], P('col')
Inputs may be any that keep to these rules, and one draw needn't show every extreme that they name: `reflectors`: each panel's vectors are dense and linearly independent. factors[k] is the upper triangular compact WY factor of reflectors[k]: its inverse plus its inverse's transpose equals reflectors[k]^T reflectors[k], so that I - reflectors[k] factors[k] reflectors[k]^T is orthogonal up to rounding.
All inputs are finite; a program needn't handle non-finite values.
Results may differ from a plain program's by a relative error of at most 0.014.
Values may be sent and summed in bfloat16 or wider, within the bound.
No kernel may reach another device: no remote copies, remote signals or barrier semaphores. Data moves between devices by JAX's collectives and lax.ppermute only.
A program may use at most 64 MiB of HBM per device.

v0:
```python
import jax
import jax.numpy as jnp
from jax import lax
from jax.sharding import PartitionSpec as P

NORD = 49152


def from_everyone(value, axis):
    copies = jnp.broadcast_to(value, (lax.axis_size(axis), *value.shape))
    return lax.all_to_all(copies, axis, split_axis=0, concat_axis=0, tiled=True)


def taken_together(value, axis):
    everything = from_everyone(value, axis)
    return jnp.sum(everything, axis=0)


def body(eigvecs, reflectors, factors):
    vectors = eigvecs
    panels = reflectors.shape[0]
    width = reflectors.shape[2]
    local_rows = reflectors.shape[1]
    stacked = jnp.transpose(reflectors, (1, 0, 2)).reshape(local_rows, panels * width)
    local_proj = lax.dot_general(
        stacked, eigvecs, (((0,), (0,)), ((), ())), preferred_element_type=jnp.float32
    )
    local_gram = lax.dot_general(
        stacked, stacked, (((0,), (0,)), ((), ())), preferred_element_type=jnp.float32
    )
    total_proj, total_gram = (
        lax.psum(local_proj.astype(jnp.bfloat16), "row").astype(jnp.float32),
        lax.psum(local_gram.astype(jnp.bfloat16), "row").astype(jnp.float32),
    )
    earlier = []
    for panel in range(panels):
        proj = total_proj[panel * width : (panel + 1) * width]
        for prior in range(panel):
            cross = total_gram[
                panel * width : (panel + 1) * width, prior * width : (prior + 1) * width
            ]
            proj = proj - jnp.dot(
                cross, earlier[prior].astype(jnp.float32), precision=lax.Precision.HIGHEST
            )
        scaled = jnp.dot(factors[panel], proj, precision=lax.Precision.HIGHEST).astype(jnp.bfloat16)
        earlier.append(scaled)
        update = jnp.dot(reflectors[panel], scaled, preferred_element_type=jnp.float32)
        vectors = (vectors.astype(jnp.float32) - update).astype(jnp.bfloat16)
    wide = vectors.astype(jnp.float32)
    local_squares = jnp.sum(wide * wide, axis=0)
    squares = taken_together(local_squares, "row")
    deviation = jnp.sqrt(squares / NORD) - 1.0
    return (vectors, deviation)


def solution(mesh):
    placed = (P("row", "col"), P(None, "row", None), P())
    return jax.shard_map(
        body, mesh=mesh, in_specs=placed, out_specs=(P("row", "col"), P("col")), check_vma=False
    )
```

profile of v0, /device:TPU:1, one launch (start us, length us, event | category | flops | bytes accessed | tf_op | source)
XLA Modules:
  0.0 208.2 jit_solution(14584094052297874776)
XLA Ops:
  7.2 4.6 %copy.14 = bf16[8,1536,128]{1,2,0:T(8,128)(2,1)} copy(bf16[8,1536,128]{2,1,0:T(8,128)(2,1)} %param.4) | data formatting | bytes 6291456 | tf_op args[1]
  11.8 7.7 %convolution_convert_fusion = bf16[1024,1024]{1,0:T(8,128)(2,1)} fusion(bf16[1536,1024]{0,1:T(8,128)(2,1)} %bitcast.132), kind=kOutput, calls=%fused_computation.17 | convolution fusion | flops 3222274048 | bytes 5242880 | tf_op jit(solution)/shard_map/dot_general | solution.py:28
  19.6 4.6 %convolution_convert_fusion.1 = bf16[1024,1024]{1,0:T(8,128)(2,1)} fusion(bf16[1536,1024]{0,1:T(8,128)(2,1)S(1)} %bitcast.133, bf16[1536,1024]{1,0:T(8,128)(2,1)S(1)} %copy-done.1), kind=kOutput, calls=%fused_computation.18 | convolution fusion | flops 3222274048 | bytes 8388608 | tf_op jit(solution)/shard_map/dot_general | solution.py:25
  24.2 3.4 %copy.13 = bf16[1536,1024]{0,1:T(8,128)(2,1)S(1)} copy(bf16[1536,1024]{1,0:T(8,128)(2,1)} %param.3) | data formatting | bytes 6291456 | tf_op args[0]
  27.6 111.7 %all-reduce.3.cloned.1.call-done = (bf16[1024,1024]{1,0:T(8,128)(2,1)}, bf16[1024,1024]{1,0:T(8,128)(2,1)}) async-done(((bf16[1024,1024]{1,0:T(8,128)(2,1)}, bf16[1024,1024]{1,0:T(8,128)(2,1)}), (bf16[1024,1024]{1,0:T(8,128)(2,1)}, bf16[1024,1024]{1,0:T(8,128)(2,1)})) %all-reduce.3.cloned.1.call-update) | async-done | bytes 4194320 | tf_op jit(solution)/shard_map/psum | solution.py:32
  139.3 2.1 convert_element_type.126
  141.4 1.4 convolution_convert_fusion.9
  142.8 1.0 convolution_subtract_fusion.6
  149.8 1.0 convolution_convert_fusion.8
  150.8 1.0 convolution_subtract_fusion.5
  151.8 1.0 convolution_subtract_fusion.25
  152.8 1.0 convolution_convert_fusion.7
  153.8 1.0 convolution_subtract_fusion.23
  156.8 1.0 convolution_convert_fusion.6
  161.7 1.0 convolution_convert_fusion.5
  167.7 1.0 convolution_convert_fusion.4
  172.7 1.1 convolution_subtract_fusion.1
  174.9 1.0 convolution_convert_fusion.3
  176.9 1.0 convolution_convert_fusion.2
  177.9 1.2 fusion.7
  185.1 1.2 multiply_reduce_fusion
  187.0 6.0 %all-to-all-start = ((f32[32,1,1024]{2,1,0:T(1,128)}), f32[32,1,1024]{2,1,0:T(1,128)S(1)}, u32[]{:S(2)}, u32[]{:S(2)}) async-start(f32[32,1,1024]{2,1,0:T(1,128)} %broadcast_in_dim.3), calls=%async_computation | async-start | bytes 262144 | tf_op jit(solution)/shard_map/all_to_all | solution.py:11
  192.9 2.9 %copy.16 = bf16[1536,1024]{1,0:T(8,128)(2,1)} copy(bf16[1536,1024]{0,1:T(8,128)(2,1)S(1)} %get-tuple-element.13) | data formatting | bytes 6291456
  195.8 4.8 %all-to-all-done = f32[32,1,1024]{2,1,0:T(1,128)S(1)} async-done(((f32[32,1,1024]{2,1,0:T(1,128)}), f32[32,1,1024]{2,1,0:T(1,128)S(1)}, u32[]{:S(2)}, u32[]{:S(2)}) %all-to-all-start) | async-done | bytes 131104 | tf_op jit(solution)/shard_map/all_to_all | solution.py:11
  (42 shorter events, 30.1 us)
Async XLA Ops:
  7.2 132.2 %all-reduce.3.cloned.1.call-start = ((), (), s32[]{:S(2)}) async-start(), calls=%async_computation.1 | async-start | bytes 8388608 | tf_op jit(solution)/shard_map/psum | solution.py:32
  11.8 7.7 %copy-start.1 = (bf16[1536,1024]{1,0:T(8,128)(2,1)S(1)}, bf16[1536,1024]{1,0:T(8,128)(2,1)}, u32[]{:S(2)}) copy-start(bf16[1536,1024]{1,0:T(8,128)(2,1)} %param.3) | copy-start | bytes 9437188
  11.8 7.7 %copy-start.2 = (bf16[8,1536,128]{1,2,0:T(8,128)(2,1)S(1)}, bf16[8,1536,128]{1,2,0:T(8,128)(2,1)}, u32[]{:S(2)}) copy-start(bf16[8,1536,128]{1,2,0:T(8,128)(2,1)} %copy.14) | copy-start | bytes 9437188
  139.3 2.1 %copy-start.3 = (f32[8,128,128]{2,1,0:T(8,128)S(1)}, f32[8,128,128]{2,1,0:T(8,128)}, u32[]{:S(2)}) copy-start(f32[8,128,128]{2,1,0:T(8,128)} %param.5) | copy-start | bytes 1572868
  172.7 5.2 %copy-start = (bf16[8,1536,128]{2,1,0:T(8,128)(2,1)S(1)}, bf16[8,1536,128]{2,1,0:T(8,128)(2,1)}, u32[]{:S(2)}) copy-start(bf16[8,1536,128]{2,1,0:T(8,128)(2,1)} %param.4) | copy-start | bytes 9437188
  187.0 13.6 %all-to-all-start = ((f32[32,1,1024]{2,1,0:T(1,128)}), f32[32,1,1024]{2,1,0:T(1,128)S(1)}, u32[]{:S(2)}, u32[]{:S(2)}) async-start(f32[32,1,1024]{2,1,0:T(1,128)} %broadcast_in_dim.3), calls=%async_computation | async-start | bytes 262144 | tf_op jit(solution)/shard_map/all_to_all | solution.py:11
Sparse Core Ops, SparseCore 0:
  24.3 114.9 all-reduce.2
where the time goes:
time: 210 us; the launch traced here: 208 us
  waiting for transfers between devices  117 us (56%)
  matrix products  56.8 us (27%)
  between operations  14.4 us (7%)
  local copies, waits for them, and re-layouts  11.6 us (6%)
  starting transfers between devices  5.99 us (3%)
  other arithmetic  2.78 us (1%)
    psum x1, waiting for transfers between devices, body(): lax.psum(local_proj.astype(jnp.bfloat16), 'row').astype(jnp.float32)  112 us
    dot_general x28, matrix products, body(): jnp.dot(cross, earlier[prior].astype(jnp.float32), precision=lax.Precisio...  27.8 us
    unnamed x11, local copies, waits for them, and re-layouts  10.9 us
    dot_general x8, matrix products, body(): jnp.dot(factors[panel], proj, precision=lax.Precision.HIGHEST)  8.36 us
    dot_general x8, matrix products, body(): jnp.dot(reflectors[panel], scaled, preferred_element_type=jnp.float32)  8.32 us
    dot_general x1, matrix products, body(): lax.dot_general(stacked, stacked, (((0,), (0,)), ((), ())), preferred_ele...  7.74 us
    all_to_all x1, starting transfers between devices, from_everyone(): return lax.all_to_all(copies, axis, split_axis=0, concat_axis=0, tiled=True)  5.95 us
    all_to_all x1, waiting for transfers between devices, from_everyone(): return lax.all_to_all(copies, axis, split_axis=0, concat_axis=0, tiled=True)  4.82 us
  transfers between devices with their start and end apart: 2, of which 2 were waited for; matrix products, arithmetic and copies ran while one was open for 3% of the time, Pallas kernels for 0%

commit v1 on v0

v1 whole, which is shorter than its diff:
```python
import functools

import jax
import jax.numpy as jnp
from jax import lax
from jax.experimental import pallas as pl
from jax.experimental.pallas import tpu as pltpu
from jax.sharding import Mesh
from jax.sharding import PartitionSpec as P

NORD = 49152
WIDTH = 128
PANELS = 8
CHIPS = 16
OWN = 32
HALF = CHIPS * OWN
SHARE = 112
PAIRS = PANELS * (PANELS - 1) // 2
BF = jnp.bfloat16
F32 = jnp.float32
CHIP = ("x", "z")
ROW = ("x", "z", "core")
VMEM = pl.BlockSpec(memory_space=pltpu.VMEM)
SMEM = pl.BlockSpec(memory_space=pltpu.SMEM)


def call(kernel, out_shape, in_specs, out_specs, flops, nbytes, limit=24, **kw):
    return pl.pallas_call(
        kernel,
        out_shape=out_shape,
        in_specs=in_specs,
        out_specs=out_specs,
        compiler_params=pltpu.CompilerParams(vmem_limit_bytes=limit * 2**20),
        cost_estimate=pl.CostEstimate(flops=flops, bytes_accessed=nbytes, transcendentals=0),
        **kw,
    )


def first_block(k):
    return k * (k - 1) // 2


def gram_kernel(v_ref, g_ref):
    for j in range(0, PANELS - 1, 2):
        left = jnp.concatenate([v_ref[j], v_ref[j + 1]], axis=1)
        for k in range(j + 1, PANELS, 2):
            right = v_ref[k]
            if k + 1 < PANELS:
                right = jnp.concatenate([right, v_ref[k + 1]], axis=1)
            both = lax.dot_general(
                left, right, (((0,), (0,)), ((), ())), preferred_element_type=F32
            ).astype(BF)
            for dj in range(2):
                for dk in range(right.shape[1] // WIDTH):
                    jj, kk = j + dj, k + dk
                    if jj < kk:
                        at = (first_block(kk) + jj) * WIDTH
                        g_ref[at : at + WIDTH, :] = both[
                            dj * WIDTH : (dj + 1) * WIDTH, dk * WIDTH : (dk + 1) * WIDTH
                        ]


def proj_kernel(flip, core_ref, x_ref, v_ref, p_ref):
    half = core_ref[0]
    if flip:
        half = 1 - half
    step = 256
    for n in range(0, HALF, step):
        at = pl.multiple_of(half * HALF + n, step)
        x = x_ref[:, pl.ds(at, step)]
        xt = x.T
        for k in range(0, PANELS, 2):
            right = jnp.concatenate([v_ref[k], v_ref[k + 1]], axis=1)
            both = jnp.dot(xt, right, preferred_element_type=F32).astype(p_ref.dtype)
            first = n // OWN
            for dk in range(2):
                p_ref[first : first + step // OWN, (k + dk) * OWN : (k + dk + 1) * OWN, :] = both[
                    :, dk * WIDTH : (dk + 1) * WIDTH
                ].reshape(step // OWN, OWN, WIDTH)


def combine_kernel(own_ref, other_ref, g_ref, out_ref):
    share = g_ref[0].astype(F32)
    for r in range(1, 2 * CHIPS):
        share = share + g_ref[r].astype(F32)
    share = share.astype(BF)
    for s in range(CHIPS):
        out_ref[s, : PANELS * OWN, :] = (own_ref[s] + other_ref[s].astype(F32)).astype(BF)
        out_ref[s, PANELS * OWN :, :] = share


def solve_kernel(core_ref, mine_ref, theirs_ref, t_ref, out_ref, g_ref):
    core = core_ref[0]
    for s in range(CHIPS):
        at = pl.multiple_of((2 * s + core) * SHARE, 16)
        g_ref[pl.ds(at, SHARE), :] = mine_ref[s, PANELS * OWN :, :]
        at = pl.multiple_of((2 * s + 1 - core) * SHARE, 16)
        g_ref[pl.ds(at, SHARE), :] = theirs_ref[s]
    done = []
    for k in range(PANELS):
        rows = slice(k * OWN, (k + 1) * OWN)
        proj = mine_ref[0, rows, :].astype(F32)
        for s in range(1, CHIPS):
            proj = proj + mine_ref[s, rows, :].astype(F32)
        if k:
            at = first_block(k) * WIDTH
            cross = g_ref[at : at + k * WIDTH, :]
            before = jnp.concatenate(done, axis=1) if k > 1 else done[0]
            proj = proj - jnp.dot(before, cross, preferred_element_type=F32)
        scaled = lax.dot_general(
            proj,
            t_ref[k],
            (((1,), (1,)), ((), ())),
            precision=lax.Precision.HIGHEST,
            preferred_element_type=F32,
        ).astype(BF)
        done.append(scaled)
        for s in range(CHIPS):
            out_ref[s, rows, :] = scaled


def update_kernel(half_ref, x_ref, v_ref, s_ref, *refs):
    out_ref, sq_ref = refs[-2:]
    left = jnp.concatenate([v_ref[k] for k in range(PANELS)], axis=1)
    right = jnp.concatenate(
        [s_ref[:, k * OWN : (k + 1) * OWN, :].reshape(HALF, WIDTH) for k in range(PANELS)], axis=1
    )
    update = lax.dot_general(left, right, (((1,), (1,)), ((), ())), preferred_element_type=F32)
    out = (x_ref[...].astype(F32) - update).astype(BF)
    out_ref[...] = out
    wide = out.astype(F32)
    squares = jnp.sum(wide * wide, axis=0, keepdims=True)

    @pl.when(pl.program_id(0) == 0)
    def _():
        sq_ref[...] = squares

    @pl.when(pl.program_id(0) > 0)
    def _():
        sq_ref[...] += squares


def update(half, eigvecs, reflectors, scaled, so_far=None):
    rows, columns = eigvecs.shape
    block = 256
    in_specs = [
        pl.BlockSpec((block, HALF), lambda i, h: (i, h[0])),
        pl.BlockSpec((PANELS, block, WIDTH), lambda i, h: (0, i, 0)),
        pl.BlockSpec((CHIPS, PANELS * OWN, WIDTH), lambda i, h: (0, 0, 0)),
    ]
    args = [half, eigvecs, reflectors, scaled]
    aliases = {}
    if so_far is not None:
        in_specs.append(pl.BlockSpec(memory_space=pl.ANY))
        args.append(so_far)
        aliases = {4: 0}
    return pl.pallas_call(
        update_kernel,
        out_shape=(
            jax.ShapeDtypeStruct((rows, columns), BF),
            jax.ShapeDtypeStruct((1, HALF), F32),
        ),
        grid_spec=pltpu.PrefetchScalarGridSpec(
            num_scalar_prefetch=1,
            grid=(rows // block,),
            in_specs=in_specs,
            out_specs=(
                pl.BlockSpec((block, HALF), lambda i, h: (i, h[0])),
                pl.BlockSpec((1, HALF), lambda i, h: (0, 0)),
            ),
        ),
        input_output_aliases=aliases,
        compiler_params=pltpu.CompilerParams(
            vmem_limit_bytes=24 * 2**20, dimension_semantics=("arbitrary",)
        ),
        cost_estimate=pl.CostEstimate(
            flops=2 * rows * HALF * PANELS * WIDTH, bytes_accessed=6 * 2**20, transcendentals=0
        ),
    )(*args)


def swapped(value):
    return lax.ppermute(value, "core", [(0, 1), (1, 0)])


def exchanged(value, axes):
    return lax.all_to_all(value, axes, split_axis=0, concat_axis=0, tiled=True)


def body(eigvecs, reflectors, factors):
    rows = eigvecs.shape[0]
    core = lax.axis_index("core").astype(jnp.int32).reshape(1)
    flops = 2 * rows * HALF * PANELS * WIDTH
    gram = call(
        gram_kernel, jax.ShapeDtypeStruct((PAIRS * WIDTH, WIDTH), BF), [VMEM], VMEM, flops, 4 * 2**20
    )(reflectors)
    gram_parts = exchanged(gram.reshape(2 * CHIPS, SHARE, WIDTH), ROW)

    def proj(flip, dtype):
        return call(
            functools.partial(proj_kernel, flip),
            jax.ShapeDtypeStruct((CHIPS, PANELS * OWN, WIDTH), dtype),
            [SMEM, VMEM, VMEM],
            VMEM,
            flops,
            6 * 2**20,
        )(core, eigvecs, reflectors)

    other = swapped(proj(True, BF))
    own = proj(False, F32)
    payload = call(
        combine_kernel,
        jax.ShapeDtypeStruct((CHIPS, PANELS * OWN + SHARE, WIDTH), BF),
        [VMEM] * 3,
        VMEM,
        2**20,
        4 * 2**20,
    )(own, other, gram_parts)
    mine = exchanged(payload, CHIP)
    theirs = swapped(mine[:, PANELS * OWN :, :])
    scaled = call(
        solve_kernel,
        jax.ShapeDtypeStruct((CHIPS, PANELS * OWN, WIDTH), BF),
        [SMEM] + [VMEM] * 3,
        VMEM,
        2**26,
        4 * 2**20,
        scratch_shapes=[pltpu.VMEM((PAIRS * WIDTH, WIDTH), BF)],
    )(core, mine, theirs, factors)
    scaled_mine = exchanged(scaled, CHIP)
    scaled_theirs = swapped(scaled_mine)
    vectors, squares_mine = update(core, eigvecs, reflectors, scaled_mine)
    vectors, squares_theirs = update(1 - core, eigvecs, reflectors, scaled_theirs, vectors)
    both = jnp.concatenate([squares_mine, squares_theirs], axis=0)
    first = core[0] == 0
    local = jnp.where(first, both, both[::-1]).reshape(1, -1)
    everything = exchanged(jnp.broadcast_to(local, (2 * CHIPS, local.shape[1])), ROW)
    deviation = jnp.sqrt(jnp.sum(everything, axis=0) / NORD) - 1.0
    return (vectors, deviation)


def solution(mesh):
    split = Mesh(mesh.devices.reshape(4, 4, 2, 4), ("x", "z", "core", "col"))
    placed = (P(ROW, "col"), P(None, ROW, None), P())
    return jax.shard_map(
        body, mesh=split, in_specs=placed, out_specs=(P(ROW, "col"), P("col")), check_vma=False
    )
```

time: 210 us -> 117 us (0.56)
  waiting for transfers between devices: 117 us -> 12 us
  matrix products: 56.8 us -> 0 us
  blocking collectives: 0 us -> 54.6 us
  Pallas kernels: 0 us -> 23.1 us
  between operations: 14.4 us -> 0.77 us
  starting transfers between devices: 5.99 us -> 13.6 us
    psum x1 -> x0, waiting for transfers between devices: 112 us -> none  [body(): lax.psum(local_proj.astype(jnp.bfloat16), 'row').astype(jnp.float32)]
    dot_general x46 -> x0, matrix products: 56.8 us -> none  [the longest x28 27.8 us: body(): jnp.dot(cross, earlier[prior].astype(jnp.float32), precision=lax.Precisio...]
    all_to_all x0 -> x3, blocking collectives: none -> 54.6 us  [exchanged(): return lax.all_to_all(value, axes, split_axis=0, concat_axis=0, tiled=True)]
    pallas_call x0 -> x7, Pallas kernels: none -> 23.1 us  [the longest x2 11.3 us: update(): pl.pallas_call(update_kernel, out_shape=(jax.ShapeDtypeStruct((rows, colu...]
    all_to_all x1, waiting for transfers between devices: 4.82 us -> 10.5 us  [exchanged(): return lax.all_to_all(value, axes, split_axis=0, concat_axis=0, tiled=True)]
    ppermute x0 -> x3, starting transfers between devices: none -> 5.43 us  [swapped(): return lax.ppermute(value, 'core', [(0, 1), (1, 0)])]
    all_to_all x1, starting transfers between devices: 5.95 us -> 8.2 us  [exchanged(): return lax.all_to_all(value, axes, split_axis=0, concat_axis=0, tiled=True)]
    unnamed x11 -> x21, local copies, waits for them, and re-layouts: 10.9 us -> 11.4 us
  transfers between devices with their start and end apart: 2 -> 4, of which waited for: 2 -> 2; matrix products, arithmetic and copies ran while one was open for 3% -> 0% of each run, Pallas kernels for 0% -> 8%
where the time goes in v1:
time: 117 us; the launch traced here: 116 us
  blocking collectives  54.6 us (47%)
  Pallas kernels  23.1 us (20%)
  starting transfers between devices  13.6 us (12%)
  waiting for transfers between devices  12 us (10%)
  local copies, waits for them, and re-layouts  11.6 us (10%)
    all_to_all x3, blocking collectives, exchanged(): return lax.all_to_all(value, axes, split_axis=0, concat_axis=0, tiled=True)  54.6 us
    unnamed x21, local copies, waits for them, and re-layouts  11.4 us
    pallas_call x2, Pallas kernels, update(): pl.pallas_call(update_kernel, out_shape=(jax.ShapeDtypeStruct((rows, colu...  11.3 us
    all_to_all x1, waiting for transfers between devices, exchanged(): return lax.all_to_all(value, axes, split_axis=0, concat_axis=0, tiled=True)  10.5 us
    all_to_all x1, starting transfers between devices, exchanged(): return lax.all_to_all(value, axes, split_axis=0, concat_axis=0, tiled=True)  8.2 us
    ppermute x3, starting transfers between devices, swapped(): return lax.ppermute(value, 'core', [(0, 1), (1, 0)])  5.43 us
    pallas_call x2, Pallas kernels, proj(): call(functools.partial(proj_kernel, flip), jax.ShapeDtypeStruct((CHIPS, P...  4.66 us
    pallas_call x1, Pallas kernels, body(): call(solve_kernel, jax.ShapeDtypeStruct((CHIPS, PANELS * OWN, WIDTH), BF)...  3.14 us
  transfers between devices with their start and end apart: 4, of which 2 were waited for; matrix products, arithmetic and copies ran while one was open for 0% of the time, Pallas kernels for 8%

profile of v1, /device:TPU:1, one launch (start us, length us, event | category | flops | bytes accessed | tf_op | source)
XLA Modules:
  0.0 116.4 jit_solution(12954194499943095528)
XLA Ops:
  0.6 1.9 %copy-done = bf16[1536,1024]{1,0:T(8,128)(2,1)S(1)} copy-done((bf16[1536,1024]{1,0:T(8,128)(2,1)S(1)}, bf16[1536,1024]{1,0:T(8,128)(2,1)}, u32[]{:S(2)}) %copy-start) | copy-done | bytes 3145752
  2.5 1.9 %copy-done.2 = bf16[8,1536,128]{2,1,0:T(8,128)(2,1)S(1)} copy-done((bf16[8,1536,128]{2,1,0:T(8,128)(2,1)S(1)}, bf16[8,1536,128]{2,1,0:T(8,128)(2,1)}, u32[]{:S(2)}) %copy-start.2) | copy-done | bytes 3145752
  4.4 2.8 %shard_map.51 = bf16[16,256,128]{2,1,0:T(8,128)(2,1)} custom-call(s32[1]{0:T(128)} %bitcast.core_ref.half_ref, bf16[1536,1024]{1,0:T(8,128)(2,1)S(1)} %copy-done, bf16[8,1536,128]{2,1,0:T(8,128)(2,1)S(1)} %copy-done.2), custom_call_target="tpu_custom_call" | custom-call | flops 1610612736 | bytes 6291456 | tf_op jit(solution)/shard_map/pallas_call | solution.py:200
  7.2 1.4 %collective-permute-start = (bf16[16,256,128]{2,1,0:T(8,128)(2,1)}, bf16[16,256,128]{2,1,0:T(8,128)(2,1)}, u32[]{:S(2)}, u32[]{:S(2)}) collective-permute-start(bf16[16,256,128]{2,1,0:T(8,128)(2,1)} %shard_map.51), channel_id=1, source_target_pairs={{0,4},{4,0},{1,5},{5,1},{2,6},{6,2},{3,7},{7,3},{8,12},{12,8},{9,1... | collective-permute-start | bytes 3145736 | tf_op jit(solution)/shard_map/ppermute | solution.py:183
  8.6 2.2 %shard_map.52 = bf16[3584,128]{1,0:T(8,128)(2,1)S(1)} custom-call(bf16[8,1536,128]{2,1,0:T(8,128)(2,1)S(1)} %copy-done.3), custom_call_target="tpu_custom_call" | custom-call | flops 1610612736 | bytes 4194304 | tf_op jit(solution)/shard_map/pallas_call | solution.py:194
  10.9 0.9 copy-done.8
  11.8 8.2 %all-to-all-start = ((bf16[32,112,128]{2,1,0:T(8,128)(2,1)}), bf16[32,112,128]{2,1,0:T(8,128)(2,1)}, u32[]{:S(2)}, u32[]{:S(2)}) async-start(bf16[32,112,128]{2,1,0:T(8,128)(2,1)} %bitcast.5), calls=%async_computation | async-start | bytes 1835008 | tf_op jit(solution)/shard_map/all_to_all | solution.py:187
  20.1 1.9 %copy-done.4 = bf16[8,1536,128]{2,1,0:T(8,128)(2,1)S(1)} copy-done((bf16[8,1536,128]{2,1,0:T(8,128)(2,1)S(1)}, bf16[8,1536,128]{2,1,0:T(8,128)(2,1)}, u32[]{:S(2)}) %copy-start.4) | copy-done | bytes 3145752
  21.9 1.8 %shard_map.50.own_ref = f32[16,256,128]{2,1,0:T(8,128)S(1)} custom-call(s32[1]{0:T(128)} %bitcast.core_ref.half_ref, bf16[1536,1024]{1,0:T(8,128)(2,1)S(1)} %copy-done.1, bf16[8,1536,128]{2,1,0:T(8,128)(2,1)S(1)} %copy-done.4), custom_call_target="tpu_custom_call" | custom-call | flops 1610612736 | bytes 6291456 | tf_op jit(solution)/shard_map/pallas_call | solution.py:200
  23.8 1.3 %copy-done.6 = f32[16,256,128]{2,1,0:T(8,128)} copy-done((f32[16,256,128]{2,1,0:T(8,128)}, f32[16,256,128]{2,1,0:T(8,128)S(1)}, u32[]{:S(2)}) %copy-start.6) | copy-done | bytes 2097176
  25.1 10.5 %all-to-all-done.g_ref = bf16[32,112,128]{2,1,0:T(8,128)(2,1)} async-done(((bf16[32,112,128]{2,1,0:T(8,128)(2,1)}), bf16[32,112,128]{2,1,0:T(8,128)(2,1)}, u32[]{:S(2)}, u32[]{:S(2)}) %all-to-all-start) | async-done | bytes 917536 | tf_op jit(solution)/shard_map/all_to_all | solution.py:187
  35.6 1.6 %copy-done.7 = f32[16,256,128]{2,1,0:T(8,128)S(1)} copy-done((f32[16,256,128]{2,1,0:T(8,128)S(1)}, f32[16,256,128]{2,1,0:T(8,128)}, u32[]{:S(2)}) %copy-start.7) | copy-done | bytes 2097176
  37.2 1.8 %shard_map.53 = bf16[16,368,128]{2,1,0:T(8,128)(2,1)S(1)} custom-call(f32[16,256,128]{2,1,0:T(8,128)S(1)} %copy-done.7, bf16[16,256,128]{2,1,0:T(8,128)(2,1)} %collective-permute-done.other_ref, bf16[32,112,128]{2,1,0:T(8,128)(2,1)} %all-to-all-done.g_ref), custom_call_target="tpu_custom_call" | custom-call | flops 1048576 | bytes 4194304 | tf_op jit(solution)/shard_map/pallas_call | solution.py:211
  39.0 24.1 %all_to_all.21.mine_ref = bf16[16,368,128]{2,1,0:T(8,128)(2,1)S(1)} all-to-all(bf16[16,368,128]{2,1,0:T(8,128)(2,1)S(1)} %shard_map.53), channel_id=1, replica_groups=mesh['x'=4,'z'=4,'core'=2,'col'=4] {'x','z'}, dimensions={0} | all-to-all | bytes 3014656 | tf_op jit(solution)/shard_map/all_to_all | solution.py:187
  63.2 2.0 %collective-permute-start.1 = (bf16[16,112,128]{2,1,0:T(8,128)(2,1)S(1)}, bf16[16,112,128]{2,1,0:T(8,128)(2,1)S(1)}, u32[]{:S(2)}, u32[]{:S(2)}) collective-permute-start(bf16[16,112,128]{2,1,0:T(8,128)(2,1)S(1)} %slice.4), channel_id=1, source_target_pairs={{0,4},{4,0},{1,5},{5,1},{2,6},{6,2},{3,7},{7,3},{8,12},{12,8},{9,1... | collective-permute-start | bytes 1376264 | tf_op jit(solution)/shard_map/ppermute | solution.py:183
  65.2 1.4 %collective-permute-done.1.theirs_ref = bf16[16,112,128]{2,1,0:T(8,128)(2,1)S(1)} collective-permute-done((bf16[16,112,128]{2,1,0:T(8,128)(2,1)S(1)}, bf16[16,112,128]{2,1,0:T(8,128)(2,1)S(1)}, u32[]{:S(2)}, u32[]{:S(2)}) %collective-permute-start.1) | collective-permute-done | bytes 458784 | tf_op jit(solution)/shard_map/ppermute | solution.py:183
  66.7 3.1 %shard_map.54 = bf16[16,256,128]{2,1,0:T(8,128)(2,1)S(1)} custom-call(s32[1]{0:T(128)} %bitcast.core_ref.half_ref, bf16[16,368,128]{2,1,0:T(8,128)(2,1)S(1)} %all_to_all.21.mine_ref, bf16[16,112,128]{2,1,0:T(8,128)(2,1)S(1)} %collective-permute-done.1.theirs_ref, f32[8,128,128]{2,1,0:T(8,128)S(1)} %copy-done.9), custom_call_target="tpu_custom_call" | custom-call | flops 67108864 | bytes 4194304 | tf_op jit(solution)/shard_map/pallas_call | solution.py:221
  69.8 19.3 %all_to_all.22.s_ref = bf16[16,256,128]{2,1,0:T(8,128)(2,1)} all-to-all(bf16[16,256,128]{2,1,0:T(8,128)(2,1)S(1)} %shard_map.54), channel_id=1, replica_groups=mesh['x'=4,'z'=4,'core'=2,'col'=4] {'x','z'}, dimensions={0} | all-to-all | bytes 2097152 | tf_op jit(solution)/shard_map/all_to_all | solution.py:187
  89.2 2.0 %collective-permute-start.2 = (bf16[16,256,128]{2,1,0:T(8,128)(2,1)}, bf16[16,256,128]{2,1,0:T(8,128)(2,1)}, u32[]{:S(2)}, u32[]{:S(2)}) collective-permute-start(bf16[16,256,128]{2,1,0:T(8,128)(2,1)} %all_to_all.22.s_ref), channel_id=1, source_target_pairs={{0,4},{4,0},{1,5},{5,1},{2,6},{6,2},{3,7},{7,3},{8,12},{12,8},{9,1... | collective-permute-start | bytes 3145736 | tf_op jit(solution)/shard_map/ppermute | solution.py:183
  91.2 1.9 %copy-done.5 = bf16[8,1536,128]{2,1,0:T(8,128)(2,1)S(1)} copy-done((bf16[8,1536,128]{2,1,0:T(8,128)(2,1)S(1)}, bf16[8,1536,128]{2,1,0:T(8,128)(2,1)}, u32[]{:S(2)}) %copy-start.5) | copy-done | bytes 3145752
  93.1 5.6 %shard_map.55 = (bf16[1536,1024]{1,0:T(8,128)(2,1)}, f32[1,512]{1,0:T(1,128)S(1)}) custom-call(s32[1]{0:T(128)} %bitcast.core_ref.half_ref, bf16[1536,1024]{1,0:T(8,128)(2,1)S(1)} %copy-done.1, bf16[8,1536,128]{2,1,0:T(8,128)(2,1)S(1)} %copy-done.5, bf16[16,256,128]{2,1,0:T(8,128)(2,1)} %all_to_all.22.s_ref), custom_call_target="tpu_custom_call" | custom-call | flops 1610612736 | bytes 6291456 | tf_op jit(solution)/shard_map/pallas_call | solution.py:157
  98.7 5.6 %shard_map.56 = (bf16[1536,1024]{1,0:T(8,128)(2,1)}, f32[1,512]{1,0:T(1,128)S(1)}) custom-call(s32[1]{0:T(128)S(6)} %sub.7.half_ref, bf16[1536,1024]{1,0:T(8,128)(2,1)S(1)} %copy-done.1, bf16[8,1536,128]{2,1,0:T(8,128)(2,1)S(1)} %copy-done.5, bf16[16,256,128]{2,1,0:T(8,128)(2,1)} %collective-permute-done.2.s_ref, ...), custom_call_target="tpu_custom_call", output_to_operand_aliasing={{0}: (4, {})} | custom-call | flops 1610612736 | bytes 6291456 | tf_op jit(solution)/shard_map/pallas_call | solution.py:157
  104.6 11.1 %all_to_all.23 = f32[32,1,1024]{2,1,0:T(1,128)S(1)} all-to-all(f32[32,1,1024]{2,1,0:T(1,128)S(1)} %broadcast_in_dim.8), channel_id=1, replica_groups=mesh['x'=4,'z'=4,'core'=2,'col'=4] {'x','z','core'}, dimensions={0} | all-to-all | bytes 262144 | tf_op jit(solution)/shard_map/all_to_all | solution.py:187
  115.8 0.6 sqrt_add_fusion
  (22 shorter events, 0.4 us)
Async XLA Ops:
  0.6 1.9 %copy-start = (bf16[1536,1024]{1,0:T(8,128)(2,1)S(1)}, bf16[1536,1024]{1,0:T(8,128)(2,1)}, u32[]{:S(2)}) copy-start(bf16[1536,1024]{1,0:T(8,128)(2,1)} %x_ref.7) | copy-start | bytes 9437188
  2.5 1.9 %copy-start.2 = (bf16[8,1536,128]{2,1,0:T(8,128)(2,1)S(1)}, bf16[8,1536,128]{2,1,0:T(8,128)(2,1)}, u32[]{:S(2)}) copy-start(bf16[8,1536,128]{2,1,0:T(8,128)(2,1)} %v_ref.9) | copy-start | bytes 9437188
  4.4 4.2 %copy-start.3 = (bf16[8,1536,128]{2,1,0:T(8,128)(2,1)S(1)}, bf16[8,1536,128]{2,1,0:T(8,128)(2,1)}, u32[]{:S(2)}) copy-start(bf16[8,1536,128]{2,1,0:T(8,128)(2,1)} %v_ref.9) | copy-start | bytes 9437188
  7.2 12.8 %copy-start.1 = (bf16[1536,1024]{1,0:T(8,128)(2,1)S(1)}, bf16[1536,1024]{1,0:T(8,128)(2,1)}, u32[]{:S(2)}) copy-start(bf16[1536,1024]{1,0:T(8,128)(2,1)} %x_ref.7) | copy-start | bytes 9437188
  7.2 28.4 %collective-permute-start = (bf16[16,256,128]{2,1,0:T(8,128)(2,1)}, bf16[16,256,128]{2,1,0:T(8,128)(2,1)}, u32[]{:S(2)}, u32[]{:S(2)}) collective-permute-start(bf16[16,256,128]{2,1,0:T(8,128)(2,1)} %shard_map.51), channel_id=1, source_target_pairs={{0,4},{4,0},{1,5},{5,1},{2,6},{6,2},{3,7},{7,3},{8,12},{12,8},{9,1... | collective-permute-start | bytes 3145736 | tf_op jit(solution)/shard_map/ppermute | solution.py:183
  10.9 0.9 copy-start.8
  11.8 23.8 %all-to-all-start = ((bf16[32,112,128]{2,1,0:T(8,128)(2,1)}), bf16[32,112,128]{2,1,0:T(8,128)(2,1)}, u32[]{:S(2)}, u32[]{:S(2)}) async-start(bf16[32,112,128]{2,1,0:T(8,128)(2,1)} %bitcast.5), calls=%async_computation | async-start | bytes 1835008 | tf_op jit(solution)/shard_map/all_to_all | solution.py:187
  20.0 1.9 %copy-start.4 = (bf16[8,1536,128]{2,1,0:T(8,128)(2,1)S(1)}, bf16[8,1536,128]{2,1,0:T(8,128)(2,1)}, u32[]{:S(2)}) copy-start(bf16[8,1536,128]{2,1,0:T(8,128)(2,1)} %v_ref.9) | copy-start | bytes 9437188
  23.8 1.3 %copy-start.6 = (f32[16,256,128]{2,1,0:T(8,128)}, f32[16,256,128]{2,1,0:T(8,128)S(1)}, u32[]{:S(2)}) copy-start(f32[16,256,128]{2,1,0:T(8,128)S(1)} %shard_map.50.own_ref) | copy-start | bytes 6291460
  35.6 1.6 %copy-start.7 = (f32[16,256,128]{2,1,0:T(8,128)S(1)}, f32[16,256,128]{2,1,0:T(8,128)}, u32[]{:S(2)}) copy-start(f32[16,256,128]{2,1,0:T(8,128)} %copy-done.6) | copy-start | bytes 6291460
  39.0 27.6 %copy-start.9 = (f32[8,128,128]{2,1,0:T(8,128)S(1)}, f32[8,128,128]{2,1,0:T(8,128)}, u32[]{:S(2)}) copy-start(f32[8,128,128]{2,1,0:T(8,128)} %t_ref.1) | copy-start | bytes 1572868
  63.2 3.5 %collective-permute-start.1 = (bf16[16,112,128]{2,1,0:T(8,128)(2,1)S(1)}, bf16[16,112,128]{2,1,0:T(8,128)(2,1)S(1)}, u32[]{:S(2)}, u32[]{:S(2)}) collective-permute-start(bf16[16,112,128]{2,1,0:T(8,128)(2,1)S(1)} %slice.4), channel_id=1, source_target_pairs={{0,4},{4,0},{1,5},{5,1},{2,6},{6,2},{3,7},{7,3},{8,12},{12,8},{9,1... | collective-permute-start | bytes 1376264 | tf_op jit(solution)/shard_map/ppermute | solution.py:183
  89.2 9.5 %collective-permute-start.2 = (bf16[16,256,128]{2,1,0:T(8,128)(2,1)}, bf16[16,256,128]{2,1,0:T(8,128)(2,1)}, u32[]{:S(2)}, u32[]{:S(2)}) collective-permute-start(bf16[16,256,128]{2,1,0:T(8,128)(2,1)} %all_to_all.22.s_ref), channel_id=1, source_target_pairs={{0,4},{4,0},{1,5},{5,1},{2,6},{6,2},{3,7},{7,3},{8,12},{12,8},{9,1... | collective-permute-start | bytes 3145736 | tf_op jit(solution)/shard_map/ppermute | solution.py:183
  91.2 1.9 %copy-start.5 = (bf16[8,1536,128]{2,1,0:T(8,128)(2,1)S(1)}, bf16[8,1536,128]{2,1,0:T(8,128)(2,1)}, u32[]{:S(2)}) copy-start(bf16[8,1536,128]{2,1,0:T(8,128)(2,1)} %v_ref.9) | copy-start | bytes 9437188

commit v2 on v1

v2 whole, which is shorter than its diff:
```python
import functools

import jax
import jax.numpy as jnp
from jax import lax
from jax.experimental import pallas as pl
from jax.experimental.pallas import tpu as pltpu
from jax.sharding import Mesh
from jax.sharding import PartitionSpec as P

NORD = 49152
WIDTH = 128
PANELS = 8
CHIPS = 16
OWN = 32
HALF = CHIPS * OWN
COLS = 4
SHARE = 32
PAIRS = PANELS * (PANELS - 1) // 2
FULL = 52
BF = jnp.bfloat16
F32 = jnp.float32
CHIP = ("x", "z")
ROW = ("x", "z", "core")
VMEM = pl.BlockSpec(memory_space=pltpu.VMEM)
SMEM = pl.BlockSpec(memory_space=pltpu.SMEM)
HBM = pl.BlockSpec(memory_space=pltpu.HBM)


def call(kernel, out_shape, in_specs, out_specs, flops, nbytes, limit=12, **kw):
    return pl.pallas_call(
        kernel,
        out_shape=out_shape,
        in_specs=in_specs,
        out_specs=out_specs,
        compiler_params=pltpu.CompilerParams(vmem_limit_bytes=limit * 2**20),
        cost_estimate=pl.CostEstimate(flops=flops, bytes_accessed=nbytes, transcendentals=0),
        **kw,
    )


def first_block(k):
    return k * (k - 1) // 2


def block_plan():
    twos, ones = [], []
    for j in range(PANELS - 1):
        ks = list(range(j + 1, PANELS))
        while len(ks) > 1:
            twos.append((j, ks.pop(0), ks.pop(0)))
        ones.extend((j, k, k) for k in ks)
    return [twos[3 * c : 3 * c + 3] + [ones[c]] for c in range(COLS)]


PLAN = block_plan()


def load(source, target, sem):
    copy = pltpu.make_async_copy(source, target, sem)
    copy.start()
    return copy


def gram_kernel(col_ref, v_hbm, g_ref, v_ref, sems):
    copies = [load(v_hbm.at[k], v_ref.at[k], sems.at[k]) for k in range(PANELS)]
    for copy in copies:
        copy.wait()
    col = col_ref[0]
    for i in range(COLS):
        index = [jnp.int32(PLAN[COLS - 1][i][n]) for n in range(3)]
        for c in range(COLS - 1):
            index = [jnp.where(col == c, PLAN[c][i][n], index[n]) for n in range(3)]
        j, k, l = index
        right = jnp.concatenate([v_ref[k], v_ref[l]], axis=1)
        both = jnp.dot(v_ref[j].T, right, preferred_element_type=F32).astype(BF)
        g_ref[2 * i * WIDTH : (2 * i + 1) * WIDTH, :] = both[:, :WIDTH]
        g_ref[(2 * i + 1) * WIDTH : (2 * i + 2) * WIDTH, :] = both[:, WIDTH:]


def share_kernel(g_ref, out_ref):
    share = g_ref[0].astype(F32)
    for r in range(1, 2 * CHIPS):
        share = share + g_ref[r].astype(F32)
    for c in range(COLS):
        out_ref[c] = share.astype(BF)


def proj_kernel(flip, core_ref, x_hbm, v_hbm, after_ref, p_ref, x_ref, v_ref, x_sems, v_sems):
    half = core_ref[0]
    if flip:
        half = 1 - half
    step = x_ref.shape[2]
    tiles = HALF // step

    def load_tile(n):
        at = pl.multiple_of(half * HALF + n * step, step)
        return load(x_hbm.at[:, pl.ds(at, step)], x_ref.at[n], x_sems.at[n])

    x_copies = [load_tile(0)]
    v_copies = [load(v_hbm.at[k], v_ref.at[k], v_sems.at[k]) for k in range(PANELS)]
    x_copies += [load_tile(n) for n in range(1, tiles)]
    for n in range(tiles):
        x_copies[n].wait()
        xt = x_ref[n].T
        for k in range(0, PANELS, 2):
            if n == 0:
                v_copies[k].wait()
                v_copies[k + 1].wait()
            right = jnp.concatenate([v_ref[k], v_ref[k + 1]], axis=1)
            both = jnp.dot(xt, right, preferred_element_type=F32).astype(p_ref.dtype)
            chips = slice(n * step // OWN, (n + 1) * step // OWN)
            for dk in range(2):
                p_ref[chips, (k + dk) * OWN : (k + dk + 1) * OWN, :] = both[
                    :, dk * WIDTH : (dk + 1) * WIDTH
                ].reshape(step // OWN, OWN, WIDTH)


def combine_kernel(own_ref, other_ref, g_ref, out_ref):
    for s in range(CHIPS):
        out_ref[s, : PANELS * OWN, :] = (own_ref[s].astype(F32) + other_ref[s].astype(F32)).astype(BF)
        for c in range(COLS):
            at = PANELS * OWN + c * SHARE
            out_ref[s, at : at + SHARE, :] = g_ref[c]


def solve_kernel(core_ref, mine_ref, theirs_ref, t_ref, out_ref, g_ref):
    core = core_ref[0]
    for c in range(COLS):
        for s in range(CHIPS):
            j, *ks = PLAN[c][s // 4]
            k = ks[s // 2 % 2]
            if s // 4 == 3 and s // 2 % 2:
                continue
            base = (first_block(k) + j) * WIDTH + s % 2 * 2 * SHARE
            rows = slice(c * SHARE, (c + 1) * SHARE)
            g_ref[pl.ds(pl.multiple_of(base + core * SHARE, SHARE), SHARE), :] = mine_ref[
                s, PANELS * OWN + c * SHARE : PANELS * OWN + (c + 1) * SHARE, :
            ]
            g_ref[pl.ds(pl.multiple_of(base + (1 - core) * SHARE, SHARE), SHARE), :] = theirs_ref[
                s, rows, :
            ]
    done = []
    for k in range(PANELS):
        rows = slice(k * OWN, (k + 1) * OWN)
        proj = mine_ref[0, rows, :].astype(F32)
        for s in range(1, CHIPS):
            proj = proj + mine_ref[s, rows, :].astype(F32)
        if k:
            at = first_block(k) * WIDTH
            cross = g_ref[at : at + k * WIDTH, :]
            before = jnp.concatenate(done, axis=1) if k > 1 else done[0]
            proj = proj - jnp.dot(before, cross, preferred_element_type=F32)
        scaled = lax.dot_general(
            proj,
            t_ref[k],
            (((1,), (1,)), ((), ())),
            precision=lax.Precision.HIGHEST,
            preferred_element_type=F32,
        ).astype(BF)
        done.append(scaled)
        for s in range(CHIPS):
            out_ref[s, rows, :] = scaled


def update_kernel(half_ref, x_hbm, v_hbm, s_ref, *refs):
    out_hbm, sq_ref, x_ref, v_ref, out_ref, sems, out_sems = refs[-7:]
    blocks = x_ref.shape[0]
    block = x_ref.shape[1]
    step = 256
    columns = pl.ds(pl.multiple_of(half_ref[0] * HALF, HALF), HALF)
    copies = []
    for i in range(blocks):
        rows = slice(i * block, (i + 1) * block)
        copies.append(
            [
                load(v_hbm.at[:, rows, :], v_ref.at[i], sems.at[2 * i]),
                load(x_hbm.at[rows, columns], x_ref.at[i], sems.at[2 * i + 1]),
            ]
        )
    squares = [jnp.zeros((1, step), F32)] * (HALF // step)
    stores = []
    for i in range(blocks):
        for copy in copies[i]:
            copy.wait()
        left = jnp.concatenate([v_ref[i, k] for k in range(PANELS)], axis=1)
        for n in range(0, HALF, step):
            chips = slice(n // OWN, (n + step) // OWN)
            right = jnp.concatenate(
                [
                    s_ref[chips, k * OWN : (k + 1) * OWN, :].reshape(step, WIDTH)
                    for k in range(PANELS)
                ],
                axis=1,
            )
            update = lax.dot_general(
                left, right, (((1,), (1,)), ((), ())), preferred_element_type=F32
            )
            out = (x_ref[i, :, n : n + step].astype(F32) - update).astype(BF)
            out_ref[i, :, n : n + step] = out
            wide = out.astype(F32)
            squares[n // step] += jnp.sum(wide * wide, axis=0, keepdims=True)
        rows = slice(i * block, (i + 1) * block)
        stores.append(load(out_ref.at[i], out_hbm.at[rows, columns], out_sems.at[i]))
    sq_ref[...] = jnp.concatenate(squares, axis=1)
    for store in stores:
        store.wait()


def update(half, eigvecs, reflectors, scaled, so_far=None):
    rows, columns = eigvecs.shape
    blocks = 3
    in_specs = [SMEM, HBM, HBM, VMEM]
    args = [half, eigvecs, reflectors, scaled]
    aliases = {}
    if so_far is not None:
        in_specs.append(HBM)
        args.append(so_far)
        aliases = {4: 0}
    return call(
        update_kernel,
        (
            jax.ShapeDtypeStruct((rows, columns), BF),
            jax.ShapeDtypeStruct((1, HALF), F32),
        ),
        in_specs,
        (HBM, VMEM),
        2 * rows * HALF * PANELS * WIDTH,
        6 * 2**20,
        limit=FULL,
        input_output_aliases=aliases,
        scratch_shapes=[
            pltpu.VMEM((blocks, rows // blocks, HALF), BF),
            pltpu.VMEM((blocks, PANELS, rows // blocks, WIDTH), BF),
            pltpu.VMEM((blocks, rows // blocks, HALF), BF),
            pltpu.SemaphoreType.DMA((2 * blocks,)),
            pltpu.SemaphoreType.DMA((blocks,)),
        ],
    )(*args)


def swapped(value):
    return lax.ppermute(value, "core", [(0, 1), (1, 0)])


def exchanged(value, axes):
    return lax.all_to_all(value, axes, split_axis=0, concat_axis=0, tiled=True)


def steps(eigvecs, reflectors, factors):
    rows = eigvecs.shape[0]
    core = lax.axis_index("core").astype(jnp.int32).reshape(1)
    flops = 2 * rows * HALF * PANELS * WIDTH
    col = lax.axis_index("col").astype(jnp.int32).reshape(1)
    gram = call(
        gram_kernel,
        jax.ShapeDtypeStruct((2 * COLS * WIDTH, WIDTH), BF),
        [SMEM, HBM],
        VMEM,
        flops // 2,
        4 * 2**20,
        limit=FULL,
        scratch_shapes=[
            pltpu.VMEM(reflectors.shape, BF),
            pltpu.SemaphoreType.DMA((PANELS,)),
        ],
    )(col, reflectors)
    gram_parts = exchanged(gram.reshape(2 * CHIPS, SHARE, WIDTH), ROW)
    share = call(
        share_kernel,
        jax.ShapeDtypeStruct((COLS, SHARE, WIDTH), BF),
        [VMEM],
        VMEM,
        2**18,
        2**18,
    )(gram_parts)
    shares = exchanged(share, "col")

    def proj(flip):
        step = 256
        return call(
            functools.partial(proj_kernel, flip),
            jax.ShapeDtypeStruct((CHIPS, PANELS * OWN, WIDTH), BF),
            [SMEM, HBM, HBM, HBM],
            VMEM,
            flops,
            6 * 2**20,
            limit=FULL,
            scratch_shapes=[
                pltpu.VMEM((HALF // step, rows, step), BF),
                pltpu.VMEM(reflectors.shape, BF),
                pltpu.SemaphoreType.DMA((HALF // step,)),
                pltpu.SemaphoreType.DMA((PANELS,)),
            ],
        )(core, eigvecs, reflectors, gram)

    other = proj(True)
    other = swapped(other)
    own = proj(False)
    payload = call(
        combine_kernel,
        jax.ShapeDtypeStruct((CHIPS, PANELS * OWN + COLS * SHARE, WIDTH), BF),
        [VMEM] * 3,
        VMEM,
        2**20,
        4 * 2**20,
    )(own, other, shares)
    mine = exchanged(payload, CHIP)
    theirs = swapped(mine[:, PANELS * OWN :, :])
    scaled = call(
        solve_kernel,
        jax.ShapeDtypeStruct((CHIPS, PANELS * OWN, WIDTH), BF),
        [SMEM] + [VMEM] * 3,
        VMEM,
        2**26,
        4 * 2**20,
        scratch_shapes=[pltpu.VMEM((PAIRS * WIDTH, WIDTH), BF)],
    )(core, mine, theirs, factors)
    scaled_mine = exchanged(scaled, CHIP)
    scaled_theirs = swapped(scaled_mine)
    vectors, squares_mine = update(core, eigvecs, reflectors, scaled_mine)
    vectors, squares_theirs = update(1 - core, eigvecs, reflectors, scaled_theirs, vectors)
    both = jnp.concatenate([squares_mine, squares_theirs], axis=0)
    first = core[0] == 0
    local = jnp.where(first, both, both[::-1]).reshape(1, -1)
    everything = exchanged(jnp.broadcast_to(local, (2 * CHIPS, local.shape[1])), ROW)
    deviation = jnp.sqrt(jnp.sum(everything, axis=0) / NORD) - 1.0
    return (vectors, deviation)


def solution(mesh):
    split = Mesh(mesh.devices.reshape(4, 4, 2, 4), ("x", "z", "core", "col"))
    placed = (P(ROW, "col"), P(None, ROW, None), P())
    return jax.shard_map(
        steps, mesh=split, in_specs=placed, out_specs=(P(ROW, "col"), P("col")), check_vma=False
    )
```

time: 117 us -> 112 us (0.957)
  blocking collectives: 54.6 us -> 71.6 us
  local copies, waits for them, and re-layouts: 11.6 us -> 0.25 us
  waiting for transfers between devices: 12 us -> 1.54 us
  starting transfers between devices: 13.6 us -> 9.75 us
  Pallas kernels: 23.1 us -> 26.8 us
    all_to_all x3 -> x4, blocking collectives: 54.6 us -> 71.6 us  [exchanged(): return lax.all_to_all(value, axes, split_axis=0, concat_axis=0, tiled=True)]
    unnamed x21 -> x3, local copies, waits for them, and re-layouts: 11.4 us -> 0.01 us
    all_to_all x1, waiting for transfers between devices: 10.5 us -> 0.01 us  [exchanged(): return lax.all_to_all(value, axes, split_axis=0, concat_axis=0, tiled=True)]
    pallas_call x2, Pallas kernels: 4.66 us -> 10.9 us  [proj(): call(functools.partial(proj_kernel, flip), jax.ShapeDtypeStruct((CHIPS, P...]
    all_to_all x1, starting transfers between devices: 8.2 us -> 4.18 us  [exchanged(): return lax.all_to_all(value, axes, split_axis=0, concat_axis=0, tiled=True)]
    pallas_call x5 -> x6, Pallas kernels: 18.4 us -> 15.9 us  [the longest x2 9.27 us: update(): call(update_kernel, (jax.ShapeDtypeStruct((rows, columns), BF), jax.Shape...]
  transfers between devices with their start and end apart: 4 -> 4, of which waited for: 2 -> 1; matrix products, arithmetic and copies ran while one was open for 0% -> 0% of each run, Pallas kernels for 8% -> 10%
where the time goes in v2:
time: 112 us; the launch traced here: 111 us
  blocking collectives  71.6 us (64%)
  Pallas kernels  26.8 us (24%)
  starting transfers between devices  9.75 us (9%)
  waiting for transfers between devices  1.54 us (1%)
    all_to_all x4, blocking collectives, exchanged(): return lax.all_to_all(value, axes, split_axis=0, concat_axis=0, tiled=True)  71.6 us
    pallas_call x2, Pallas kernels, proj(): call(functools.partial(proj_kernel, flip), jax.ShapeDtypeStruct((CHIPS, P...  10.9 us
    pallas_call x2, Pallas kernels, update(): call(update_kernel, (jax.ShapeDtypeStruct((rows, columns), BF), jax.Shape...  9.27 us
    ppermute x3, starting transfers between devices, swapped(): return lax.ppermute(value, 'core', [(0, 1), (1, 0)])  5.57 us
    all_to_all x1, starting transfers between devices, exchanged(): return lax.all_to_all(value, axes, split_axis=0, concat_axis=0, tiled=True)  4.18 us
    pallas_call x1, Pallas kernels, steps(): call(solve_kernel, jax.ShapeDtypeStruct((CHIPS, PANELS * OWN, WIDTH), BF)...  3.14 us
    pallas_call x1, Pallas kernels, steps(): call(gram_kernel, jax.ShapeDtypeStruct((2 * COLS * WIDTH, WIDTH), BF), [S...  2.62 us
  transfers between devices with their start and end apart: 4, of which 1 were waited for; matrix products, arithmetic and copies ran while one was open for 0% of the time, Pallas kernels for 10%

profile of v2, /device:TPU:1, one launch (start us, length us, event | category | flops | bytes accessed | tf_op | source)
XLA Modules:
  0.0 111.4 jit_solution(13271133793938942286)
XLA Ops:
  0.6 2.6 %shard_map.50.after_ref = bf16[1024,128]{1,0:T(8,128)(2,1)S(1)} custom-call(s32[1]{0:T(128)} %bitcast.1.col_ref, bf16[8,1536,128]{2,1,0:T(8,128)(2,1)} %v_hbm.9), custom_call_target="tpu_custom_call" | custom-call | flops 805306368 | bytes 4194304 | tf_op jit(solution)/shard_map/pallas_call | solution.py:255
  3.3 5.4 %shard_map.52 = bf16[16,256,128]{2,1,0:T(8,128)(2,1)S(1)} custom-call(s32[1]{0:T(128)} %bitcast.core_ref.half_ref, bf16[1536,1024]{1,0:T(8,128)(2,1)} %x_hbm.7, bf16[8,1536,128]{2,1,0:T(8,128)(2,1)} %v_hbm.9, bf16[1024,128]{1,0:T(8,128)(2,1)S(1)} %shard_map.50.after_ref), custom_call_target="tpu_custom_call" | custom-call | flops 1610612736 | bytes 6291456 | tf_op jit(solution)/shard_map/pallas_call | solution.py:281
  8.7 1.5 %collective-permute-start = (bf16[16,256,128]{2,1,0:T(8,128)(2,1)S(1)}, bf16[16,256,128]{2,1,0:T(8,128)(2,1)S(1)}, u32[]{:S(2)}, u32[]{:S(2)}) collective-permute-start(bf16[16,256,128]{2,1,0:T(8,128)(2,1)S(1)} %shard_map.52), channel_id=1, source_target_pairs={{0,4},{4,0},{1,5},{5,1},{2,6},{6,2},{3,7},{7,3},{8,12},{12,8},{9,1... | collective-permute-start | bytes 3145736 | tf_op jit(solution)/shard_map/ppermute | solution.py:243
  10.1 16.9 %all_to_all.26.g_ref = bf16[32,32,128]{2,1,0:T(8,128)(2,1)S(1)} all-to-all(bf16[32,32,128]{2,1,0:T(8,128)(2,1)S(1)} %bitcast.6), channel_id=1, replica_groups=mesh['x'=4,'z'=4,'core'=2,'col'=4] {'x','z','core'}, dimensions={0} | all-to-all | bytes 524288 | tf_op jit(solution)/shard_map/all_to_all | solution.py:247
  27.1 0.7 shard_map.53
  27.7 4.2 %all-to-all-start.1 = ((bf16[4,32,128]{2,1,0:T(8,128)(2,1)}), bf16[4,32,128]{2,1,0:T(8,128)(2,1)S(1)}, u32[]{:S(2)}, u32[]{:S(2)}) async-start(bf16[4,32,128]{2,1,0:T(8,128)(2,1)} %shard_map.53), calls=%async_computation.1 | async-start | bytes 65536 | tf_op jit(solution)/shard_map/all_to_all | solution.py:247
  31.9 5.4 %shard_map.51.own_ref = bf16[16,256,128]{2,1,0:T(8,128)(2,1)S(1)} custom-call(s32[1]{0:T(128)} %bitcast.core_ref.half_ref, bf16[1536,1024]{1,0:T(8,128)(2,1)} %x_hbm.7, bf16[8,1536,128]{2,1,0:T(8,128)(2,1)} %v_hbm.9, bf16[1024,128]{1,0:T(8,128)(2,1)S(1)} %shard_map.50.after_ref), custom_call_target="tpu_custom_call" | custom-call | flops 1610612736 | bytes 6291456 | tf_op jit(solution)/shard_map/pallas_call | solution.py:281
  37.3 0.0 copy-start
  37.4 0.0 collective-permute-done.other_ref
  37.4 0.2 shard_map.54
  37.6 24.3 %all_to_all.27.mine_ref = bf16[16,384,128]{2,1,0:T(8,128)(2,1)S(1)} all-to-all(bf16[16,384,128]{2,1,0:T(8,128)(2,1)S(1)} %shard_map.54), channel_id=1, replica_groups=mesh['x'=4,'z'=4,'core'=2,'col'=4] {'x','z'}, dimensions={0} | all-to-all | bytes 3145728 | tf_op jit(solution)/shard_map/all_to_all | solution.py:247
  61.9 2.0 %collective-permute-start.1 = (bf16[16,128,128]{2,1,0:T(8,128)(2,1)S(1)}, bf16[16,128,128]{2,1,0:T(8,128)(2,1)S(1)}, u32[]{:S(2)}, u32[]{:S(2)}) collective-permute-start(bf16[16,128,128]{2,1,0:T(8,128)(2,1)S(1)} %slice.4), channel_id=1, source_target_pairs={{0,4},{4,0},{1,5},{5,1},{2,6},{6,2},{3,7},{7,3},{8,12},{12,8},{9,1... | collective-permute-start | bytes 1572872 | tf_op jit(solution)/shard_map/ppermute | solution.py:243
  64.0 1.5 %collective-permute-done.1.theirs_ref = bf16[16,128,128]{2,1,0:T(8,128)(2,1)S(1)} collective-permute-done((bf16[16,128,128]{2,1,0:T(8,128)(2,1)S(1)}, bf16[16,128,128]{2,1,0:T(8,128)(2,1)S(1)}, u32[]{:S(2)}, u32[]{:S(2)}) %collective-permute-start.1) | collective-permute-done | bytes 524320 | tf_op jit(solution)/shard_map/ppermute | solution.py:243
  65.5 3.1 %shard_map.55 = bf16[16,256,128]{2,1,0:T(8,128)(2,1)S(1)} custom-call(s32[1]{0:T(128)} %bitcast.core_ref.half_ref, bf16[16,384,128]{2,1,0:T(8,128)(2,1)S(1)} %all_to_all.27.mine_ref, bf16[16,128,128]{2,1,0:T(8,128)(2,1)S(1)} %collective-permute-done.1.theirs_ref, f32[8,128,128]{2,1,0:T(8,128)S(1)} %copy-done), custom_call_target="tpu_custom_call" | custom-call | flops 67108864 | bytes 4194304 | tf_op jit(solution)/shard_map/pallas_call | solution.py:310
  68.7 19.4 %all_to_all.28.s_ref = bf16[16,256,128]{2,1,0:T(8,128)(2,1)S(1)} all-to-all(bf16[16,256,128]{2,1,0:T(8,128)(2,1)S(1)} %shard_map.55), channel_id=1, replica_groups=mesh['x'=4,'z'=4,'core'=2,'col'=4] {'x','z'}, dimensions={0} | all-to-all | bytes 2097152 | tf_op jit(solution)/shard_map/all_to_all | solution.py:247
  88.0 2.1 %collective-permute-start.2 = (bf16[16,256,128]{2,1,0:T(8,128)(2,1)S(1)}, bf16[16,256,128]{2,1,0:T(8,128)(2,1)S(1)}, u32[]{:S(2)}, u32[]{:S(2)}) collective-permute-start(bf16[16,256,128]{2,1,0:T(8,128)(2,1)S(1)} %all_to_all.28.s_ref), channel_id=1, source_target_pairs={{0,4},{4,0},{1,5},{5,1},{2,6},{6,2},{3,7},{7,3},{8,12},{12,8},{9,1... | collective-permute-start | bytes 3145736 | tf_op jit(solution)/shard_map/ppermute | solution.py:243
  90.1 4.6 %shard_map.56 = (bf16[1536,1024]{1,0:T(8,128)(2,1)}, f32[1,512]{1,0:T(1,128)S(1)}) custom-call(s32[1]{0:T(128)} %bitcast.core_ref.half_ref, bf16[1536,1024]{1,0:T(8,128)(2,1)} %x_hbm.7, bf16[8,1536,128]{2,1,0:T(8,128)(2,1)} %v_hbm.9, bf16[16,256,128]{2,1,0:T(8,128)(2,1)S(1)} %all_to_all.28.s_ref), custom_call_target="tpu_custom_call" | custom-call | flops 1610612736 | bytes 6291456 | tf_op jit(solution)/shard_map/pallas_call | solution.py:220
  94.7 0.0 collective-permute-done.2.s_ref
  94.7 4.6 %shard_map.57 = (bf16[1536,1024]{1,0:T(8,128)(2,1)}, f32[1,512]{1,0:T(1,128)S(1)}) custom-call(s32[1]{0:T(128)S(6)} %sub.7.half_ref, bf16[1536,1024]{1,0:T(8,128)(2,1)} %x_hbm.7, bf16[8,1536,128]{2,1,0:T(8,128)(2,1)} %v_hbm.9, bf16[16,256,128]{2,1,0:T(8,128)(2,1)S(1)} %collective-permute-done.2.s_ref, ...), custom_call_target="tpu_custom_call", output_to_operand_aliasing={{0}: (4, {})} | custom-call | flops 1610612736 | bytes 6291456 | tf_op jit(solution)/shard_map/pallas_call | solution.py:220
  99.4 0.1 rev.3
  99.6 0.1 broadcast_in_dim.8
  99.6 11.1 %all_to_all.29 = f32[32,1,1024]{2,1,0:T(1,128)S(1)} all-to-all(f32[32,1,1024]{2,1,0:T(1,128)S(1)} %broadcast_in_dim.8), channel_id=1, replica_groups=mesh['x'=4,'z'=4,'core'=2,'col'=4] {'x','z','core'}, dimensions={0} | all-to-all | bytes 262144 | tf_op jit(solution)/shard_map/all_to_all | solution.py:247
  110.7 0.1 reduce_sum.9
  110.8 0.6 sqrt_add_fusion
  (6 shorter events, 0.1 us)
Async XLA Ops:
  8.7 28.7 %collective-permute-start = (bf16[16,256,128]{2,1,0:T(8,128)(2,1)S(1)}, bf16[16,256,128]{2,1,0:T(8,128)(2,1)S(1)}, u32[]{:S(2)}, u32[]{:S(2)}) collective-permute-start(bf16[16,256,128]{2,1,0:T(8,128)(2,1)S(1)} %shard_map.52), channel_id=1, source_target_pairs={{0,4},{4,0},{1,5},{5,1},{2,6},{6,2},{3,7},{7,3},{8,12},{12,8},{9,1... | collective-permute-start | bytes 3145736 | tf_op jit(solution)/shard_map/ppermute | solution.py:243
  27.7 9.6 %all-to-all-start.1 = ((bf16[4,32,128]{2,1,0:T(8,128)(2,1)}), bf16[4,32,128]{2,1,0:T(8,128)(2,1)S(1)}, u32[]{:S(2)}, u32[]{:S(2)}) async-start(bf16[4,32,128]{2,1,0:T(8,128)(2,1)} %shard_map.53), calls=%async_computation.1 | async-start | bytes 65536 | tf_op jit(solution)/shard_map/all_to_all | solution.py:247
  37.3 28.2 %copy-start = (f32[8,128,128]{2,1,0:T(8,128)S(1)}, f32[8,128,128]{2,1,0:T(8,128)}, u32[]{:S(2)}) copy-start(f32[8,128,128]{2,1,0:T(8,128)} %t_ref.1) | copy-start | bytes 1572868
  61.9 3.6 %collective-permute-start.1 = (bf16[16,128,128]{2,1,0:T(8,128)(2,1)S(1)}, bf16[16,128,128]{2,1,0:T(8,128)(2,1)S(1)}, u32[]{:S(2)}, u32[]{:S(2)}) collective-permute-start(bf16[16,128,128]{2,1,0:T(8,128)(2,1)S(1)} %slice.4), channel_id=1, source_target_pairs={{0,4},{4,0},{1,5},{5,1},{2,6},{6,2},{3,7},{7,3},{8,12},{12,8},{9,1... | collective-permute-start | bytes 1572872 | tf_op jit(solution)/shard_map/ppermute | solution.py:243
  88.0 6.7 %collective-permute-start.2 = (bf16[16,256,128]{2,1,0:T(8,128)(2,1)S(1)}, bf16[16,256,128]{2,1,0:T(8,128)(2,1)S(1)}, u32[]{:S(2)}, u32[]{:S(2)}) collective-permute-start(bf16[16,256,128]{2,1,0:T(8,128)(2,1)S(1)} %all_to_all.28.s_ref), channel_id=1, source_target_pairs={{0,4},{4,0},{1,5},{5,1},{2,6},{6,2},{3,7},{7,3},{8,12},{12,8},{9,1... | collective-permute-start | bytes 3145736 | tf_op jit(solution)/shard_map/ppermute | solution.py:243

commit v3 on v0

v3 whole, which is shorter than its diff:
```python
import functools

import jax
import jax.numpy as jnp
from jax import lax
from jax.experimental import pallas as pl
from jax.experimental.pallas import tpu as pltpu
from jax.sharding import Mesh
from jax.sharding import PartitionSpec as P

NORD = 49152
WIDTH = 128
PANELS = 8
CHIPS = 16
OWN = 32
HALF = CHIPS * OWN
PAIRS = PANELS * (PANELS - 1) // 2
SHARE = PAIRS * WIDTH // (2 * CHIPS)
PROJ = PANELS * OWN
CHUNK = PROJ + SHARE
STEP = 256
BF = jnp.bfloat16
F32 = jnp.float32
CHIP = ("x", "z")
ROW = ("x", "z", "core")
VMEM = pl.BlockSpec(memory_space=pltpu.VMEM)
HBM = pl.BlockSpec(memory_space=pltpu.HBM)


def call(kernel, out_shape, in_specs, out_specs, flops, nbytes, limit=12, **kw):
    return pl.pallas_call(
        kernel,
        out_shape=out_shape,
        in_specs=in_specs,
        out_specs=out_specs,
        compiler_params=pltpu.CompilerParams(vmem_limit_bytes=limit * 2**20),
        cost_estimate=pl.CostEstimate(flops=flops, bytes_accessed=nbytes, transcendentals=0),
        **kw,
    )


def first_block(k):
    return k * (k - 1) // 2


def load(source, target, sem):
    copy = pltpu.make_async_copy(source, target, sem)
    copy.start()
    return copy


def pair(v_ref, k):
    return jnp.concatenate([v_ref[k], v_ref[k + 1]], axis=1)


def project(x_ref, v_ref, half, p_ref, ready=None):
    for n in range(0, HALF, STEP):
        if ready is not None:
            ready(n // STEP)
        at = pl.multiple_of(half * HALF + n, STEP)
        xt = x_ref[:, pl.ds(at, STEP)].T
        chips = slice(n // OWN, (n + STEP) // OWN)
        for k in range(0, PANELS, 2):
            both = jnp.dot(xt, pair(v_ref, k), preferred_element_type=F32).astype(BF)
            for dk in range(2):
                p_ref[chips, (k + dk) * OWN : (k + dk + 1) * OWN, :] = both[
                    :, dk * WIDTH : (dk + 1) * WIDTH
                ].reshape(STEP // OWN, OWN, WIDTH)


def first_kernel(x_hbm, v_hbm, other_ref, mine_ref, x_ref, v_ref, g_ref, x_sems, v_sems):
    core = lax.axis_index("core")
    v_copies = [load(v_hbm.at[k], v_ref.at[k], v_sems.at[k]) for k in range(PANELS)]
    x_copies = []
    for i, half in enumerate((1 - core, core)):
        for n in range(0, HALF, STEP):
            at = pl.ds(pl.multiple_of(half * HALF + n, STEP), STEP)
            x_copies.append(
                load(x_hbm.at[:, at], x_ref.at[:, at], x_sems.at[i * HALF // STEP + n // STEP])
            )
    for k in range(0, PANELS, 2):
        v_copies[k].wait()
        v_copies[k + 1].wait()
        right = pair(v_ref, k)
        for j in range(0, k + 1, 2):
            both = jnp.dot(pair(v_ref, j).T, right, preferred_element_type=F32).astype(BF)
            for dj in range(2):
                for dk in range(2):
                    if j + dj < k + dk:
                        at = (first_block(k + dk) + j + dj) * WIDTH
                        g_ref[at : at + WIDTH, :] = both[
                            dj * WIDTH : (dj + 1) * WIDTH, dk * WIDTH : (dk + 1) * WIDTH
                        ]
    for s in range(CHIPS):
        at = pl.multiple_of((1 - core) * CHIPS * SHARE + s * SHARE, 16)
        other_ref[s, PROJ:, :] = g_ref[pl.ds(at, SHARE), :]
        at = pl.multiple_of(core * CHIPS * SHARE + s * SHARE, 16)
        mine_ref[s] = g_ref[pl.ds(at, SHARE), :]
    project(x_ref, v_ref, 1 - core, other_ref, ready=lambda n: x_copies[n].wait())
    for copy in x_copies[HALF // STEP :]:
        copy.wait()


def own_kernel(x_ref, v_ref, p_ref):
    project(x_ref, v_ref, lax.axis_index("core"), p_ref)


def combine_kernel(own_ref, gram_ref, other_ref, out_ref):
    for s in range(CHIPS):
        out_ref[s, :PROJ, :] = (
            own_ref[s].astype(F32) + other_ref[s, :PROJ, :].astype(F32)
        ).astype(BF)
        out_ref[s, PROJ:, :] = (
            gram_ref[s].astype(F32) + other_ref[s, PROJ:, :].astype(F32)
        ).astype(BF)


def sum_kernel(parts_ref, out_ref):
    rows = 16
    for at in range(0, CHUNK, rows):
        total = parts_ref[0, at : at + rows, :].astype(F32)
        for s in range(1, CHIPS):
            total = total + parts_ref[s, at : at + rows, :].astype(F32)
        total = total.astype(BF)
        for s in range(CHIPS):
            out_ref[s, at : at + rows, :] = total


def split(value):
    high = value.astype(BF)
    return high, (value - high.astype(F32)).astype(BF)


def solve_kernel(mine_ref, theirs_ref, t_ref, out_ref, g_ref):
    core = lax.axis_index("core")
    for s in range(CHIPS):
        at = pl.multiple_of(core * CHIPS * SHARE + s * SHARE, 16)
        g_ref[pl.ds(at, SHARE), :] = mine_ref[s, PROJ:, :]
        at = pl.multiple_of((1 - core) * CHIPS * SHARE + s * SHARE, 16)
        g_ref[pl.ds(at, SHARE), :] = theirs_ref[s]
    groups = range(0, CHIPS, CHIPS // 2)
    done = [[] for _ in groups]
    for k in range(PANELS):
        rows = slice(k * OWN, (k + 1) * OWN)
        factor, rest = split(t_ref[k])
        factor = jnp.concatenate([factor, factor, rest], axis=1)
        for i, g in enumerate(groups):
            chips = slice(g, g + CHIPS // 2)
            proj = mine_ref[chips, rows, :].reshape(HALF // 2, WIDTH).astype(F32)
            if k:
                at = first_block(k) * WIDTH
                cross = g_ref[at : at + k * WIDTH, :]
                before = jnp.concatenate(done[i], axis=1) if k > 1 else done[i][0]
                proj = proj - jnp.dot(before, cross, preferred_element_type=F32)
            high, low = split(proj)
            scaled = lax.dot_general(
                jnp.concatenate([high, low, high], axis=1),
                factor,
                (((1,), (1,)), ((), ())),
                preferred_element_type=F32,
            ).astype(BF)
            done[i].append(scaled)
            out_ref[chips, rows, :] = scaled.reshape(CHIPS // 2, OWN, WIDTH)


def update_kernel(flip, x_ref, v_ref, s_ref, *refs):
    out_hbm, sq_ref, out_ref, sems = refs[-4:]
    half = lax.axis_index("core")
    if flip:
        half = 1 - half
    blocks, block = out_ref.shape[:2]
    columns = pl.ds(pl.multiple_of(half * HALF, HALF), HALF)
    squares = [jnp.zeros((1, STEP), F32)] * (HALF // STEP)
    stores = []
    for i in range(blocks):
        rows = slice(i * block, (i + 1) * block)
        left = jnp.concatenate([v_ref[k, rows, :] for k in range(PANELS)], axis=1)
        for n in range(0, HALF, STEP):
            chips = slice(n // OWN, (n + STEP) // OWN)
            right = jnp.concatenate(
                [
                    s_ref[chips, k * OWN : (k + 1) * OWN, :].reshape(STEP, WIDTH)
                    for k in range(PANELS)
                ],
                axis=1,
            )
            update = lax.dot_general(
                left, right, (((1,), (1,)), ((), ())), preferred_element_type=F32
            )
            x = x_ref[rows, pl.ds(pl.multiple_of(half * HALF + n, STEP), STEP)]
            out = (x.astype(F32) - update).astype(BF)
            out_ref[i, :, n : n + STEP] = out
            wide = out.astype(F32)
            squares[n // STEP] += jnp.sum(wide * wide, axis=0, keepdims=True)
        stores.append(load(out_ref.at[i], out_hbm.at[rows, columns], sems.at[i]))
    squares = jnp.concatenate(squares, axis=1)
    if flip:
        for r in range(2 * CHIPS):
            sq_ref[r, :, columns] = squares
            sq_ref[r, :, pl.ds(pl.multiple_of((1 - half) * HALF, HALF), HALF)] = refs[1][...]
    else:
        sq_ref[...] = squares
    for store in stores:
        store.wait()


def update(flip, eigvecs, reflectors, scaled, *so_far):
    rows, columns = eigvecs.shape
    blocks = 3
    in_specs = [VMEM] * 3
    args = [eigvecs, reflectors, scaled]
    aliases = {}
    squares = (1, HALF)
    if flip:
        in_specs += [HBM, VMEM]
        args += so_far
        aliases = {3: 0}
        squares = (2 * CHIPS, 1, columns)
    return call(
        functools.partial(update_kernel, flip),
        (
            jax.ShapeDtypeStruct((rows, columns), BF),
            jax.ShapeDtypeStruct(squares, F32),
        ),
        in_specs,
        (HBM, VMEM),
        2 * rows * HALF * PANELS * WIDTH,
        6 * 2**20,
        input_output_aliases=aliases,
        scratch_shapes=[
            pltpu.VMEM((blocks, rows // blocks, HALF), BF),
            pltpu.SemaphoreType.DMA((blocks,)),
        ],
    )(*args)


def swapped(value):
    return lax.ppermute(value, "core", [(0, 1), (1, 0)])


def exchanged(value, axes):
    return lax.all_to_all(value, axes, split_axis=0, concat_axis=0, tiled=True)


def steps(eigvecs, reflectors, factors):
    rows = eigvecs.shape[0]
    flops = 2 * rows * HALF * PANELS * WIDTH
    chunks = jax.ShapeDtypeStruct((CHIPS, CHUNK, WIDTH), BF)
    projections = jax.ShapeDtypeStruct((CHIPS, PROJ, WIDTH), BF)
    other, gram, eigvecs, reflectors = call(
        first_kernel,
        (
            chunks,
            jax.ShapeDtypeStruct((CHIPS, SHARE, WIDTH), BF),
            pltpu.VMEM(eigvecs.shape, BF),
            pltpu.VMEM(reflectors.shape, BF),
        ),
        [HBM] * 2,
        (VMEM,) * 4,
        2 * flops,
        8 * 2**20,
        limit=54,
        scratch_shapes=[
            pltpu.VMEM((PAIRS * WIDTH, WIDTH), BF),
            pltpu.SemaphoreType.DMA((2 * HALF // STEP,)),
            pltpu.SemaphoreType.DMA((PANELS,)),
        ],
    )(eigvecs, reflectors)
    other = swapped(other)
    own = call(own_kernel, projections, [VMEM] * 2, VMEM, flops, 6 * 2**20)(
        eigvecs, reflectors
    )
    payload = call(combine_kernel, chunks, [VMEM] * 3, VMEM, 2**20, 4 * 2**20)(own, gram, other)
    parts = exchanged(payload, CHIP)
    sums = call(sum_kernel, chunks, [VMEM], VMEM, 2**20, 3 * 2**20)(parts)
    mine = exchanged(sums, CHIP)
    theirs = swapped(mine[:, PROJ:, :])
    scaled = call(
        solve_kernel,
        projections,
        [VMEM] * 3,
        VMEM,
        2**28,
        4 * 2**20,
        scratch_shapes=[pltpu.VMEM((PAIRS * WIDTH, WIDTH), BF)],
    )(mine, theirs, factors)
    scaled_theirs = swapped(scaled)
    vectors, squares_mine = update(False, eigvecs, reflectors, scaled)
    vectors, squares = update(
        True, eigvecs, reflectors, scaled_theirs, vectors, squares_mine
    )
    everything = exchanged(squares, ROW)
    deviation = jnp.sqrt(jnp.sum(everything, axis=(0, 1)) / NORD) - 1.0
    return (vectors, deviation)


def solution(mesh):
    split_mesh = Mesh(mesh.devices.reshape(4, 4, 2, 4), ("x", "z", "core", "col"))
    placed = (P(ROW, "col"), P(None, ROW, None), P())
    return jax.shard_map(
        steps, mesh=split_mesh, in_specs=placed, out_specs=(P(ROW, "col"), P("col")), check_vma=False
    )
```

time: 210 us -> 91.9 us (0.44)
  waiting for transfers between devices: 117 us -> 2.74 us
  blocking collectives: 0 us -> 63.1 us
  matrix products: 56.8 us -> 0 us
  Pallas kernels: 0 us -> 19.2 us
  between operations: 14.4 us -> 0.69 us
  local copies, waits for them, and re-layouts: 11.6 us -> 0.04 us
    psum x1 -> x0, waiting for transfers between devices: 112 us -> none  [body(): lax.psum(local_proj.astype(jnp.bfloat16), 'row').astype(jnp.float32)]
    all_to_all x0 -> x3, blocking collectives: none -> 63.1 us  [exchanged(): return lax.all_to_all(value, axes, split_axis=0, concat_axis=0, tiled=True)]
    dot_general x46 -> x0, matrix products: 56.8 us -> none  [the longest x28 27.8 us: body(): jnp.dot(cross, earlier[prior].astype(jnp.float32), precision=lax.Precisio...]
    pallas_call x0 -> x7, Pallas kernels: none -> 19.2 us  [the longest x1 7.89 us: steps(): call(first_kernel, (chunks, jax.ShapeDtypeStruct((CHIPS, SHARE, WIDTH), B...]
    unnamed x11 -> x4, local copies, waits for them, and re-layouts: 10.9 us -> 0.01 us
    all_to_all x1 -> x0, starting transfers between devices: 5.95 us -> none  [from_everyone(): return lax.all_to_all(copies, axis, split_axis=0, concat_axis=0, tiled=True)]
    ppermute x0 -> x3, starting transfers between devices: none -> 5.18 us  [swapped(): return lax.ppermute(value, 'core', [(0, 1), (1, 0)])]
    all_to_all x1 -> x0, waiting for transfers between devices: 4.82 us -> none  [from_everyone(): return lax.all_to_all(copies, axis, split_axis=0, concat_axis=0, tiled=True)]
  transfers between devices with their start and end apart: 2 -> 3, of which waited for: 2 -> 2; matrix products, arithmetic and copies ran while one was open for 3% -> 0% of each run, Pallas kernels for 0% -> 5%
where the time goes in v3:
time: 91.9 us; the launch traced here: 91.6 us
  blocking collectives  63.1 us (69%)
  Pallas kernels  19.2 us (21%)
  starting transfers between devices  5.18 us (6%)
  waiting for transfers between devices  2.74 us (3%)
    all_to_all x3, blocking collectives, exchanged(): return lax.all_to_all(value, axes, split_axis=0, concat_axis=0, tiled=True)  63.1 us
    pallas_call x1, Pallas kernels, steps(): call(first_kernel, (chunks, jax.ShapeDtypeStruct((CHIPS, SHARE, WIDTH), B...  7.89 us
    pallas_call x2, Pallas kernels, update(): call(functools.partial(update_kernel, flip), (jax.ShapeDtypeStruct((rows,...  5.51 us
    ppermute x3, starting transfers between devices, swapped(): return lax.ppermute(value, 'core', [(0, 1), (1, 0)])  5.18 us
    pallas_call x1, Pallas kernels, steps(): call(solve_kernel, projections, [VMEM] * 3, VMEM, 2 ** 28, 4 * 2 ** 20, s...  3.39 us
    ppermute x3, waiting for transfers between devices, swapped(): return lax.ppermute(value, 'core', [(0, 1), (1, 0)])  2.74 us
    pallas_call x1, Pallas kernels, steps(): call(own_kernel, projections, [VMEM] * 2, VMEM, flops, 6 * 2 ** 20)  1.85 us
  transfers between devices with their start and end apart: 3, of which 2 were waited for; matrix products, arithmetic and copies ran while one was open for 0% of the time, Pallas kernels for 5%

profile of v3, /device:TPU:1, one launch (start us, length us, event | category | flops | bytes accessed | tf_op | source)
XLA Modules:
  0.0 91.6 jit_solution(3513336729871276058)
XLA Ops:
  0.6 7.9 %shard_map.50 = (bf16[16,368,128]{2,1,0:T(8,128)(2,1)}, bf16[16,112,128]{2,1,0:T(8,128)(2,1)}, bf16[1536,1024]{1,0:T(8,128)(2,1)S(1)}, bf16[8,1536,128]{2,1,0:T(8,128)(2,1)S(1)}) custom-call(bf16[1536,1024]{1,0:T(8,128)(2,1)} %x_hbm.1, bf16[8,1536,128]{2,1,0:T(8,128)(2,1)} %v_hbm.1), custom_call_target="tpu_custom_call" | custom-call | flops 3221225472 | bytes 8388608 | tf_op jit(solution)/shard_map/pallas_call | solution.py:250
  8.5 1.5 %collective-permute-start = (bf16[16,368,128]{2,1,0:T(8,128)(2,1)}, bf16[16,368,128]{2,1,0:T(8,128)(2,1)S(1)}, u32[]{:S(2)}, u32[]{:S(2)}) collective-permute-start(bf16[16,368,128]{2,1,0:T(8,128)(2,1)} %get-tuple-element.13), channel_id=1, source_target_pairs={{0,4},{4,0},{1,5},{5,1},{2,6},{6,2},{3,7},{7,3},{8,12},{12,8},{9,1... | collective-permute-start | bytes 4521992 | tf_op jit(solution)/shard_map/ppermute | solution.py:238
  10.0 0.0 copy-start.1
  10.0 1.8 %shard_map.51.own_ref = bf16[16,256,128]{2,1,0:T(8,128)(2,1)S(1)} custom-call(bf16[1536,1024]{1,0:T(8,128)(2,1)S(1)} %get-tuple-element.10.x_ref, bf16[8,1536,128]{2,1,0:T(8,128)(2,1)S(1)} %get-tuple-element.11.v_ref), custom_call_target="tpu_custom_call" | custom-call | flops 1610612736 | bytes 6291456 | tf_op jit(solution)/shard_map/pallas_call | solution.py:270
  11.9 1.3 %collective-permute-done.other_ref = bf16[16,368,128]{2,1,0:T(8,128)(2,1)S(1)} collective-permute-done((bf16[16,368,128]{2,1,0:T(8,128)(2,1)}, bf16[16,368,128]{2,1,0:T(8,128)(2,1)S(1)}, u32[]{:S(2)}, u32[]{:S(2)}) %collective-permute-start) | collective-permute-done | bytes 1507360 | tf_op jit(solution)/shard_map/ppermute | solution.py:238
  13.2 0.0 copy-done.1
  13.2 0.3 shard_map.52
  13.5 28.5 %all_to_all.15.parts_ref = bf16[16,368,128]{2,1,0:T(8,128)(2,1)S(1)} all-to-all(bf16[16,368,128]{2,1,0:T(8,128)(2,1)S(1)} %shard_map.52), channel_id=1, replica_groups=mesh['x'=4,'z'=4,'core'=2,'col'=4] {'x','z'}, dimensions={0} | all-to-all | bytes 3014656 | tf_op jit(solution)/shard_map/all_to_all | solution.py:242
  42.1 0.0 copy-start
  42.1 0.2 shard_map.53
  42.3 23.5 %all_to_all.16.mine_ref = bf16[16,368,128]{2,1,0:T(8,128)(2,1)S(1)} all-to-all(bf16[16,368,128]{2,1,0:T(8,128)(2,1)S(1)} %shard_map.53), channel_id=1, replica_groups=mesh['x'=4,'z'=4,'core'=2,'col'=4] {'x','z'}, dimensions={0} | all-to-all | bytes 3014656 | tf_op jit(solution)/shard_map/all_to_all | solution.py:242
  65.8 3.1 %collective-permute-start.1 = (bf16[16,112,128]{2,1,0:T(8,128)(2,1)S(1)}, bf16[16,112,128]{2,1,0:T(8,128)(2,1)S(1)}, u32[]{:S(2)}, u32[]{:S(2)}) collective-permute-start(bf16[16,112,128]{2,1,0:T(8,128)(2,1)S(1)} %slice.4), channel_id=1, source_target_pairs={{0,4},{4,0},{1,5},{5,1},{2,6},{6,2},{3,7},{7,3},{8,12},{12,8},{9,1... | collective-permute-start | bytes 1376264 | tf_op jit(solution)/shard_map/ppermute | solution.py:238
  68.8 1.4 %collective-permute-done.1.theirs_ref = bf16[16,112,128]{2,1,0:T(8,128)(2,1)S(1)} collective-permute-done((bf16[16,112,128]{2,1,0:T(8,128)(2,1)S(1)}, bf16[16,112,128]{2,1,0:T(8,128)(2,1)S(1)}, u32[]{:S(2)}, u32[]{:S(2)}) %collective-permute-start.1) | collective-permute-done | bytes 458784 | tf_op jit(solution)/shard_map/ppermute | solution.py:238
  70.3 0.0 copy-done
  70.3 3.4 %shard_map.54.s_ref = bf16[16,256,128]{2,1,0:T(8,128)(2,1)S(1)} custom-call(bf16[16,368,128]{2,1,0:T(8,128)(2,1)S(1)} %all_to_all.16.mine_ref, bf16[16,112,128]{2,1,0:T(8,128)(2,1)S(1)} %collective-permute-done.1.theirs_ref, f32[8,128,128]{2,1,0:T(8,128)S(1)} %copy-done), custom_call_target="tpu_custom_call" | custom-call | flops 268435456 | bytes 4194304 | tf_op jit(solution)/shard_map/pallas_call | solution.py:278
  73.7 0.6 collective-permute-start.2
  74.3 2.8 %shard_map.55 = (bf16[1536,1024]{1,0:T(8,128)(2,1)}, f32[1,512]{1,0:T(1,128)S(1)}) custom-call(bf16[1536,1024]{1,0:T(8,128)(2,1)S(1)} %get-tuple-element.10.x_ref, bf16[8,1536,128]{2,1,0:T(8,128)(2,1)S(1)} %get-tuple-element.11.v_ref, bf16[16,256,128]{2,1,0:T(8,128)(2,1)S(1)} %shard_map.54.s_ref), custom_call_target="tpu_custom_call" | custom-call | flops 1610612736 | bytes 6291456 | tf_op jit(solution)/shard_map/pallas_call | solution.py:219
  77.1 0.0 collective-permute-done.2.s_ref
  77.1 2.8 %shard_map.56 = (bf16[1536,1024]{1,0:T(8,128)(2,1)}, f32[32,1,1024]{2,1,0:T(1,128)S(1)}) custom-call(bf16[1536,1024]{1,0:T(8,128)(2,1)S(1)} %get-tuple-element.10.x_ref, bf16[8,1536,128]{2,1,0:T(8,128)(2,1)S(1)} %get-tuple-element.11.v_ref, bf16[16,256,128]{2,1,0:T(8,128)(2,1)S(1)} %collective-permute-done.2.s_ref, ...), custom_call_target="tpu_custom_call", output_to_operand_aliasing={{0}: (3, {})} | custom-call | flops 1610612736 | bytes 6291456 | tf_op jit(solution)/shard_map/pallas_call | solution.py:219
  79.8 11.1 %all_to_all.17 = f32[32,1,1024]{2,1,0:T(1,128)S(1)} all-to-all(f32[32,1,1024]{2,1,0:T(1,128)S(1)} %get-tuple-element.17), channel_id=1, replica_groups=mesh['x'=4,'z'=4,'core'=2,'col'=4] {'x','z','core'}, dimensions={0} | all-to-all | bytes 262144 | tf_op jit(solution)/shard_map/all_to_all | solution.py:242
  90.9 0.1 reduce_sum.9
  91.0 0.6 sqrt_add_fusion
  (1 shorter events, 0.0 us)
Async XLA Ops:
  8.5 4.7 %collective-permute-start = (bf16[16,368,128]{2,1,0:T(8,128)(2,1)}, bf16[16,368,128]{2,1,0:T(8,128)(2,1)S(1)}, u32[]{:S(2)}, u32[]{:S(2)}) collective-permute-start(bf16[16,368,128]{2,1,0:T(8,128)(2,1)} %get-tuple-element.13), channel_id=1, source_target_pairs={{0,4},{4,0},{1,5},{5,1},{2,6},{6,2},{3,7},{7,3},{8,12},{12,8},{9,1... | collective-permute-start | bytes 4521992 | tf_op jit(solution)/shard_map/ppermute | solution.py:238
  10.0 3.2 %copy-start.1 = (bf16[16,112,128]{2,1,0:T(8,128)(2,1)S(1)}, bf16[16,112,128]{2,1,0:T(8,128)(2,1)}, u32[]{:S(2)}) copy-start(bf16[16,112,128]{2,1,0:T(8,128)(2,1)} %get-tuple-element.12.gram_ref) | copy-start | bytes 1376260
  42.1 28.2 %copy-start = (f32[8,128,128]{2,1,0:T(8,128)S(1)}, f32[8,128,128]{2,1,0:T(8,128)}, u32[]{:S(2)}) copy-start(f32[8,128,128]{2,1,0:T(8,128)} %t_ref.1) | copy-start | bytes 1572868
  65.8 4.5 %collective-permute-start.1 = (bf16[16,112,128]{2,1,0:T(8,128)(2,1)S(1)}, bf16[16,112,128]{2,1,0:T(8,128)(2,1)S(1)}, u32[]{:S(2)}, u32[]{:S(2)}) collective-permute-start(bf16[16,112,128]{2,1,0:T(8,128)(2,1)S(1)} %slice.4), channel_id=1, source_target_pairs={{0,4},{4,0},{1,5},{5,1},{2,6},{6,2},{3,7},{7,3},{8,12},{12,8},{9,1... | collective-permute-start | bytes 1376264 | tf_op jit(solution)/shard_map/ppermute | solution.py:238
  73.7 3.4 %collective-permute-start.2 = (bf16[16,256,128]{2,1,0:T(8,128)(2,1)S(1)}, bf16[16,256,128]{2,1,0:T(8,128)(2,1)S(1)}, u32[]{:S(2)}, u32[]{:S(2)}) collective-permute-start(bf16[16,256,128]{2,1,0:T(8,128)(2,1)S(1)} %shard_map.54.s_ref), channel_id=1, source_target_pairs={{0,4},{4,0},{1,5},{5,1},{2,6},{6,2},{3,7},{7,3},{8,12},{12,8},{9,1... | collective-permute-start | bytes 3145736 | tf_op jit(solution)/shard_map/ppermute | solution.py:238

commit v4 on v3

v4 whole, which is shorter than its diff:
```python
import functools

import jax
import jax.numpy as jnp
from jax import lax
from jax.experimental import pallas as pl
from jax.experimental.pallas import tpu as pltpu
from jax.sharding import Mesh
from jax.sharding import PartitionSpec as P

NORD = 49152
WIDTH = 128
PANELS = 8
CHIPS = 16
OWN = 32
HALF = CHIPS * OWN
PAIRS = PANELS * (PANELS - 1) // 2
BLOCKS = PAIRS + PANELS // 2
SHARE = BLOCKS * WIDTH // (2 * CHIPS)
PROJ = PANELS * OWN
MORE = PROJ + SHARE
TILE = 16
CHUNK = MORE + TILE
STEP = 256
BF = jnp.bfloat16
F32 = jnp.float32
CHIP = ("x", "z")
ROW = (*CHIP, "core")
VMEM = pl.BlockSpec(memory_space=pltpu.VMEM)
HBM = pl.BlockSpec(memory_space=pltpu.HBM)


def call(kernel, out_shape, in_specs, out_specs, flops, nbytes, limit=12, **kw):
    return pl.pallas_call(
        kernel,
        out_shape=out_shape,
        in_specs=in_specs,
        out_specs=out_specs,
        compiler_params=pltpu.CompilerParams(vmem_limit_bytes=limit * 2**20),
        cost_estimate=pl.CostEstimate(flops=flops, bytes_accessed=nbytes, transcendentals=0),
        **kw,
    )


def first_block(k):
    return k * (k - 1) // 2


def load(source, target, sem):
    copy = pltpu.make_async_copy(source, target, sem)
    copy.start()
    return copy


def pair(v_ref, k):
    return jnp.concatenate([v_ref[k], v_ref[k + 1]], axis=1)


def parts_of(value):
    parts = []
    for _ in range(3):
        part = value.astype(BF).astype(F32)
        parts.append(part)
        value = value - part
    return parts


def packed(values):
    row = lax.broadcasted_iota(jnp.int32, (TILE, WIDTH), 0)
    tile = jnp.zeros((TILE, WIDTH), F32)
    for i, value in enumerate(values):
        for j, part in enumerate(parts_of(value)):
            tile = jnp.where(row == 3 * i + j, part, tile)
    return tile.astype(BF)


def unpacked(tile, count):
    tile = tile.astype(F32)
    return [
        tile[3 * i : 3 * i + 1] + tile[3 * i + 1 : 3 * i + 2] + tile[3 * i + 2 : 3 * i + 3]
        for i in range(count)
    ]


def project(x_ref, v_ref, half, p_ref, ready=None):
    squares = []
    for n in range(0, HALF, STEP):
        if ready is not None:
            ready(n // STEP)
        x = x_ref[:, pl.ds(pl.multiple_of(half * HALF + n, STEP), STEP)]
        wide = x.astype(F32)
        squares.append(jnp.sum(wide * wide, axis=0, keepdims=True))
        xt = x.T
        chips = slice(n // OWN, (n + STEP) // OWN)
        for k in range(0, PANELS, 2):
            both = jnp.dot(xt, pair(v_ref, k), preferred_element_type=F32).astype(BF)
            for dk in range(2):
                p_ref[chips, (k + dk) * OWN : (k + dk + 1) * OWN, :] = both[
                    :, dk * WIDTH : (dk + 1) * WIDTH
                ].reshape(STEP // OWN, OWN, WIDTH)
    return jnp.concatenate(squares, axis=1)


def load_half(half, x_hbm, x_ref, sems):
    copies = []
    for n in range(0, HALF, STEP):
        at = pl.ds(pl.multiple_of(half * HALF + n, STEP), STEP)
        copies.append(load(x_hbm.at[:, at], x_ref.at[:, at], sems.at[n // STEP]))
    return copies


def group_of(values, s):
    at = s * OWN // WIDTH * WIDTH
    return values[:, at : at + WIDTH]


def first_kernel(
    x_hbm, v_hbm, other_ref, mine_ref, diag_ref, x_ref, v_ref, g_ref, x_sems, v_sems
):
    core = lax.axis_index("core")
    v_copies = [load(v_hbm.at[k], v_ref.at[k], v_sems.at[k]) for k in range(PANELS)]
    x_copies = load_half(1 - core, x_hbm, x_ref, x_sems.at[0])
    own_copies = load_half(core, x_hbm, x_ref, x_sems.at[1])
    row = lax.broadcasted_iota(jnp.int32, (WIDTH, WIDTH), 0)
    column = lax.broadcasted_iota(jnp.int32, (WIDTH, WIDTH), 1)
    diag = []
    for k in range(0, PANELS, 2):
        v_copies[k].wait()
        v_copies[k + 1].wait()
        right = pair(v_ref, k)
        for j in range(0, k + 1, 2):
            both = jnp.dot(pair(v_ref, j).T, right, preferred_element_type=F32)
            blocks = [
                [
                    both[dj * WIDTH : (dj + 1) * WIDTH, dk * WIDTH : (dk + 1) * WIDTH]
                    for dk in range(2)
                ]
                for dj in range(2)
            ]
            for dj in range(2):
                for dk in range(2):
                    if j + dj < k + dk:
                        at = (first_block(k + dk) + j + dj) * WIDTH
                        g_ref[at : at + WIDTH, :] = blocks[dj][dk].astype(BF)
            if j == k:
                at = (PAIRS + k // 2) * WIDTH
                g_ref[at : at + WIDTH, :] = jnp.where(
                    row < column, blocks[0][0], blocks[1][1]
                ).astype(BF)
                for d in range(2):
                    diag.append(
                        jnp.sum(
                            jnp.where(row == column, blocks[d][d], 0.0), axis=0, keepdims=True
                        )
                    )
    for k in range(PANELS):
        diag_ref[k : k + 1, :] = diag[k]
    for s in range(CHIPS):
        at = pl.multiple_of((1 - core) * CHIPS * SHARE + s * SHARE, 16)
        other_ref[s, PROJ:MORE, :] = g_ref[pl.ds(at, SHARE), :]
        at = pl.multiple_of(core * CHIPS * SHARE + s * SHARE, 16)
        mine_ref[s] = g_ref[pl.ds(at, SHARE), :]
    squares = project(x_ref, v_ref, 1 - core, other_ref, lambda n: x_copies[n].wait())
    for s in range(CHIPS):
        other_ref[s, MORE:, :] = packed([group_of(squares, s), diag[s % PANELS]])
    for copy in own_copies:
        copy.wait()


def own_kernel(x_ref, v_ref, p_ref, sq_ref):
    sq_ref[...] = project(x_ref, v_ref, lax.axis_index("core"), p_ref)


def combine_kernel(own_ref, sq_ref, gram_ref, diag_ref, other_ref, out_ref):
    for s in range(CHIPS):
        out_ref[s, :PROJ, :] = (
            own_ref[s].astype(F32) + other_ref[s, :PROJ, :].astype(F32)
        ).astype(BF)
        out_ref[s, PROJ:MORE, :] = (
            gram_ref[s].astype(F32) + other_ref[s, PROJ:MORE, :].astype(F32)
        ).astype(BF)
        squares, diag = unpacked(other_ref[s, MORE:, :], 2)
        k = s % PANELS
        out_ref[s, MORE:, :] = packed(
            [group_of(sq_ref[...], s) + squares, diag_ref[k : k + 1, :] + diag]
        )


def sum_kernel(parts_ref, out_ref):
    for at in range(0, MORE, TILE):
        total = parts_ref[0, at : at + TILE, :].astype(F32)
        for s in range(1, CHIPS):
            total = total + parts_ref[s, at : at + TILE, :].astype(F32)
        total = total.astype(BF)
        for s in range(CHIPS):
            out_ref[s, at : at + TILE, :] = total
    total = parts_ref[0, MORE:, :].astype(F32)
    for s in range(1, CHIPS):
        total = total + parts_ref[s, MORE:, :].astype(F32)
    tile = packed(unpacked(total, 2))
    for s in range(CHIPS):
        out_ref[s, MORE:, :] = tile


def split(value):
    high = value.astype(BF)
    return high, (value - high.astype(F32)).astype(BF)


def solve_kernel(mine_ref, theirs_ref, t_ref, out_ref, dev_ref, g_ref):
    core = lax.axis_index("core")
    for s in range(CHIPS):
        at = pl.multiple_of(core * CHIPS * SHARE + s * SHARE, 16)
        g_ref[pl.ds(at, SHARE), :] = mine_ref[s, PROJ:MORE, :]
        at = pl.multiple_of((1 - core) * CHIPS * SHARE + s * SHARE, 16)
        g_ref[pl.ds(at, SHARE), :] = theirs_ref[s]
    row = lax.broadcasted_iota(jnp.int32, (WIDTH, WIDTH), 0)
    column = lax.broadcasted_iota(jnp.int32, (WIDTH, WIDTH), 1)
    groups = range(0, CHIPS, CHIPS // 2)
    done = [[] for _ in groups]
    change = [jnp.zeros((HALF // 2, WIDTH), F32) for _ in groups]
    for k in range(PANELS):
        rows = slice(k * OWN, (k + 1) * OWN)
        factor, rest = split(t_ref[k])
        factor = jnp.concatenate([factor, factor, rest], axis=1)
        at = (PAIRS + k // 2) * WIDTH
        own = g_ref[at : at + WIDTH, :].astype(F32)
        own = jnp.where(row > column if k % 2 else row < column, 2.0 * own, 0.0).astype(BF)
        diag = unpacked(mine_ref[k, MORE:, :], 2)[1]
        for i, g in enumerate(groups):
            chips = slice(g, g + CHIPS // 2)
            proj = mine_ref[chips, rows, :].reshape(HALF // 2, WIDTH).astype(F32)
            if k:
                at = first_block(k) * WIDTH
                cross = g_ref[at : at + k * WIDTH, :]
                before = jnp.concatenate(done[i], axis=1) if k > 1 else done[i][0]
                proj = proj - jnp.dot(before, cross, preferred_element_type=F32)
            high, low = split(proj)
            scaled = lax.dot_general(
                jnp.concatenate([high, low, high], axis=1),
                factor,
                (((1,), (1,)), ((), ())),
                preferred_element_type=F32,
            ).astype(BF)
            done[i].append(scaled)
            out_ref[chips, rows, :] = scaled.reshape(CHIPS // 2, OWN, WIDTH)
            wide = scaled.astype(F32)
            change[i] += wide * (
                jnp.dot(scaled, own, preferred_element_type=F32) + wide * diag - 2.0 * proj
            )
    squares = jnp.concatenate(
        [jnp.sum(part.T, axis=0, keepdims=True) for part in change], axis=1
    )
    before = jnp.concatenate(
        [
            unpacked(mine_ref[s, MORE:, :], 2)[0]
            for s in range(0, CHIPS, WIDTH // OWN)
        ],
        axis=1,
    )
    deviation = jnp.sqrt(jnp.maximum(before + squares, 0.0) / NORD) - 1.0
    dev_ref[...] = deviation
    tile = packed([deviation[:, n : n + WIDTH] for n in range(0, HALF, WIDTH)])
    for s in range(CHIPS):
        out_ref[s, PROJ:, :] = tile


def update_kernel(flip, x_ref, v_ref, s_ref, *refs):
    half = lax.axis_index("core")
    if flip:
        _, dev_ref, out_hbm, both_ref, out_ref, sems = refs
        columns = pl.ds(pl.multiple_of(half * HALF, HALF), HALF)
        both_ref[:, columns] = dev_ref[...]
        half = 1 - half
        columns = pl.ds(pl.multiple_of(half * HALF, HALF), HALF)
        both_ref[:, columns] = jnp.concatenate(
            unpacked(s_ref[0, PROJ:, :], HALF // WIDTH), axis=1
        )
    else:
        out_hbm, out_ref, sems = refs
        columns = pl.ds(pl.multiple_of(half * HALF, HALF), HALF)
    blocks, block = out_ref.shape[:2]
    stores = []
    for i in range(blocks):
        rows = slice(i * block, (i + 1) * block)
        left = jnp.concatenate([v_ref[k, rows, :] for k in range(PANELS)], axis=1)
        for n in range(0, HALF, STEP):
            chips = slice(n // OWN, (n + STEP) // OWN)
            right = jnp.concatenate(
                [
                    s_ref[chips, k * OWN : (k + 1) * OWN, :].reshape(STEP, WIDTH)
                    for k in range(PANELS)
                ],
                axis=1,
            )
            update = lax.dot_general(
                left, right, (((1,), (1,)), ((), ())), preferred_element_type=F32
            )
            x = x_ref[rows, pl.ds(pl.multiple_of(half * HALF + n, STEP), STEP)]
            out_ref[i, :, n : n + STEP] = (x.astype(F32) - update).astype(BF)
        stores.append(load(out_ref.at[i], out_hbm.at[rows, columns], sems.at[i]))
    for store in stores:
        store.wait()


def update(flip, eigvecs, reflectors, scaled, *so_far):
    rows = eigvecs.shape[0]
    blocks = 3
    in_specs = [VMEM] * 3
    out_shape = jax.ShapeDtypeStruct(eigvecs.shape, BF)
    out_specs = HBM
    aliases = {}
    if flip:
        in_specs += [HBM, VMEM]
        aliases = {3: 0}
        out_shape = (out_shape, jax.ShapeDtypeStruct((1, 2 * HALF), F32))
        out_specs = (HBM, VMEM)
    return call(
        functools.partial(update_kernel, flip),
        out_shape,
        in_specs,
        out_specs,
        2 * rows * HALF * PANELS * WIDTH,
        6 * 2**20,
        input_output_aliases=aliases,
        scratch_shapes=[
            pltpu.VMEM((blocks, rows // blocks, HALF), BF),
            pltpu.SemaphoreType.DMA((blocks,)),
        ],
    )(eigvecs, reflectors, scaled, *so_far)


def swapped(value):
    return lax.ppermute(value, "core", [(0, 1), (1, 0)])


def exchanged(value, axes):
    return lax.all_to_all(value, axes, split_axis=0, concat_axis=0, tiled=True)


def steps(eigvecs, reflectors, factors):
    rows = eigvecs.shape[0]
    flops = 2 * rows * HALF * PANELS * WIDTH
    chunks = jax.ShapeDtypeStruct((CHIPS, CHUNK, WIDTH), BF)
    tiles = HALF // STEP
    other, gram, diag, eigvecs, reflectors = call(
        first_kernel,
        (
            chunks,
            jax.ShapeDtypeStruct((CHIPS, SHARE, WIDTH), BF),
            jax.ShapeDtypeStruct((PANELS, WIDTH), F32),
            pltpu.VMEM(eigvecs.shape, BF),
            pltpu.VMEM(reflectors.shape, BF),
        ),
        [HBM] * 2,
        (VMEM,) * 5,
        2 * flops,
        8 * 2**20,
        limit=54,
        scratch_shapes=[
            pltpu.VMEM((BLOCKS * WIDTH, WIDTH), BF),
            pltpu.SemaphoreType.DMA((2, tiles)),
            pltpu.SemaphoreType.DMA((PANELS,)),
        ],
    )(eigvecs, reflectors)
    other = swapped(other)
    own, squares = call(
        own_kernel,
        (
            jax.ShapeDtypeStruct((CHIPS, PROJ, WIDTH), BF),
            jax.ShapeDtypeStruct((1, HALF), F32),
        ),
        [VMEM] * 2,
        (VMEM,) * 2,
        flops,
        6 * 2**20,
    )(eigvecs, reflectors)
    payload = call(combine_kernel, chunks, [VMEM] * 5, VMEM, 2**20, 4 * 2**20)(
        own, squares, gram, diag, other
    )
    parts = exchanged(payload, CHIP)
    sums = call(sum_kernel, chunks, [VMEM], VMEM, 2**20, 3 * 2**20)(parts)
    mine = exchanged(sums, CHIP)
    theirs = swapped(mine[:, PROJ:MORE, :])
    scaled, dev = call(
        solve_kernel,
        (
            jax.ShapeDtypeStruct((CHIPS, PROJ + TILE, WIDTH), BF),
            jax.ShapeDtypeStruct((1, HALF), F32),
        ),
        [VMEM] * 3,
        (VMEM,) * 2,
        2**28,
        4 * 2**20,
        scratch_shapes=[pltpu.VMEM((BLOCKS * WIDTH, WIDTH), BF)],
    )(mine, theirs, factors)
    scaled_theirs = swapped(scaled)
    vectors = update(False, eigvecs, reflectors, scaled)
    vectors, deviation = update(True, eigvecs, reflectors, scaled_theirs, vectors, dev)
    return (vectors, deviation.reshape(-1))


def solution(mesh):
    split_mesh = Mesh(mesh.devices.reshape(4, 4, 2, 4), ("x", "z", "core", "col"))
    placed = (P(ROW, "col"), P(None, ROW, None), P())
    return jax.shard_map(
        steps, mesh=split_mesh, in_specs=placed, out_specs=(P(ROW, "col"), P("col")), check_vma=False
    )
```

time: 91.9 us -> 85.1 us (0.926)
  blocking collectives: 63.1 us -> 55 us
  Pallas kernels: 19.2 us -> 21.3 us
    all_to_all x3 -> x2, blocking collectives: 63.1 us -> 55 us  [exchanged(): return lax.all_to_all(value, axes, split_axis=0, concat_axis=0, tiled=True)]
    pallas_call x5, Pallas kernels: 11.1 us -> 13 us  [the longest x2 5.91 us: update(): call(functools.partial(update_kernel, flip), out_shape, in_specs, out_spe...]
where the time goes in v4:
time: 85.1 us; the launch traced here: 84.9 us
  blocking collectives  55 us (65%)
  Pallas kernels  21.3 us (25%)
  starting transfers between devices  4.84 us (6%)
  waiting for transfers between devices  3.02 us (4%)
    all_to_all x2, blocking collectives, exchanged(): return lax.all_to_all(value, axes, split_axis=0, concat_axis=0, tiled=True)  55 us
    pallas_call x1, Pallas kernels, steps(): call(first_kernel, (chunks, jax.ShapeDtypeStruct((CHIPS, SHARE, WIDTH), B...  8.05 us
    pallas_call x2, Pallas kernels, update(): call(functools.partial(update_kernel, flip), out_shape, in_specs, out_spe...  5.91 us
    ppermute x3, starting transfers between devices, swapped(): return lax.ppermute(value, 'core', [(0, 1), (1, 0)])  4.84 us
    pallas_call x1, Pallas kernels, steps(): call(solve_kernel, (jax.ShapeDtypeStruct((CHIPS, PROJ + TILE, WIDTH), BF)...  4.76 us
    ppermute x3, waiting for transfers between devices, swapped(): return lax.ppermute(value, 'core', [(0, 1), (1, 0)])  3.02 us
    pallas_call x1, Pallas kernels, steps(): call(own_kernel, (jax.ShapeDtypeStruct((CHIPS, PROJ, WIDTH), BF), jax.Sha...  1.85 us
  transfers between devices with their start and end apart: 3, of which 2 were waited for; matrix products, arithmetic and copies ran while one was open for 0% of the time, Pallas kernels for 5%

profile of v4, /device:TPU:1, one launch (start us, length us, event | category | flops | bytes accessed | tf_op | source)
XLA Modules:
  0.0 84.9 jit_solution(1874287008102209199)
XLA Ops:
  0.6 8.0 %shard_map.50 = (bf16[16,400,128]{2,1,0:T(8,128)(2,1)}, bf16[16,128,128]{2,1,0:T(8,128)(2,1)}, f32[8,128]{1,0:T(8,128)}, bf16[1536,1024]{1,0:T(8,128)(2,1)S(1)}, bf16[8,1536,128]{2,1,0:T(8,128)(2,1)S(1)}) custom-call(bf16[1536,1024]{1,0:T(8,128)(2,1)} %x_hbm.1, bf16[8,1536,128]{2,1,0:T(8,128)(2,1)} %v_hbm.1), custom_call_target="tpu_custom_call" | custom-call | flops 3221225472 | bytes 8388608 | tf_op jit(solution)/shard_map/pallas_call | solution.py:346
  8.7 1.5 %collective-permute-start = (bf16[16,400,128]{2,1,0:T(8,128)(2,1)}, bf16[16,400,128]{2,1,0:T(8,128)(2,1)S(1)}, u32[]{:S(2)}, u32[]{:S(2)}) collective-permute-start(bf16[16,400,128]{2,1,0:T(8,128)(2,1)} %get-tuple-element.19), channel_id=1, source_target_pairs={{0,4},{4,0},{1,5},{5,1},{2,6},{6,2},{3,7},{7,3},{8,12},{12,8},{9,1... | collective-permute-start | bytes 4915208 | tf_op jit(solution)/shard_map/ppermute | solution.py:334
  10.1 0.0 copy-start
  10.1 0.0 copy-start.2
  10.1 1.9 %shard_map.51 = (bf16[16,256,128]{2,1,0:T(8,128)(2,1)S(1)}, f32[1,512]{1,0:T(1,128)S(1)}) custom-call(bf16[1536,1024]{1,0:T(8,128)(2,1)S(1)} %get-tuple-element.13.x_ref, bf16[8,1536,128]{2,1,0:T(8,128)(2,1)S(1)} %get-tuple-element.14.v_ref), custom_call_target="tpu_custom_call" | custom-call | flops 1610612736 | bytes 6291456 | tf_op jit(solution)/shard_map/pallas_call | solution.py:367
  12.0 1.5 %collective-permute-done.other_ref = bf16[16,400,128]{2,1,0:T(8,128)(2,1)S(1)} collective-permute-done((bf16[16,400,128]{2,1,0:T(8,128)(2,1)}, bf16[16,400,128]{2,1,0:T(8,128)(2,1)S(1)}, u32[]{:S(2)}, u32[]{:S(2)}) %collective-permute-start) | collective-permute-done | bytes 1638432 | tf_op jit(solution)/shard_map/ppermute | solution.py:334
  13.5 0.0 copy-done
  13.5 0.0 copy-done.2
  13.5 0.5 shard_map.52
  13.9 30.3 %all_to_all.10.parts_ref = bf16[16,400,128]{2,1,0:T(8,128)(2,1)S(1)} all-to-all(bf16[16,400,128]{2,1,0:T(8,128)(2,1)S(1)} %shard_map.52), channel_id=1, replica_groups=mesh['x'=4,'z'=4,'core'=2,'col'=4] {'x','z'}, dimensions={0} | all-to-all | bytes 3276800 | tf_op jit(solution)/shard_map/all_to_all | solution.py:338
  44.2 0.2 shard_map.53
  44.4 0.0 copy-start.1
  44.4 24.8 %all_to_all.11.mine_ref = bf16[16,400,128]{2,1,0:T(8,128)(2,1)S(1)} all-to-all(bf16[16,400,128]{2,1,0:T(8,128)(2,1)S(1)} %shard_map.53), channel_id=1, replica_groups=mesh['x'=4,'z'=4,'core'=2,'col'=4] {'x','z'}, dimensions={0} | all-to-all | bytes 3276800 | tf_op jit(solution)/shard_map/all_to_all | solution.py:338
  69.3 2.9 %collective-permute-start.1 = (bf16[16,128,128]{2,1,0:T(8,128)(2,1)S(1)}, bf16[16,128,128]{2,1,0:T(8,128)(2,1)S(1)}, u32[]{:S(2)}, u32[]{:S(2)}) collective-permute-start(bf16[16,128,128]{2,1,0:T(8,128)(2,1)S(1)} %slice.4), channel_id=1, source_target_pairs={{0,4},{4,0},{1,5},{5,1},{2,6},{6,2},{3,7},{7,3},{8,12},{12,8},{9,1... | collective-permute-start | bytes 1572872 | tf_op jit(solution)/shard_map/ppermute | solution.py:334
  72.2 1.5 %collective-permute-done.1.theirs_ref = bf16[16,128,128]{2,1,0:T(8,128)(2,1)S(1)} collective-permute-done((bf16[16,128,128]{2,1,0:T(8,128)(2,1)S(1)}, bf16[16,128,128]{2,1,0:T(8,128)(2,1)S(1)}, u32[]{:S(2)}, u32[]{:S(2)}) %collective-permute-start.1) | collective-permute-done | bytes 524320 | tf_op jit(solution)/shard_map/ppermute | solution.py:334
  73.8 0.0 copy-done.1
  73.8 4.8 %shard_map.54 = (bf16[16,272,128]{2,1,0:T(8,128)(2,1)S(1)}, f32[1,512]{1,0:T(1,128)S(1)}) custom-call(bf16[16,400,128]{2,1,0:T(8,128)(2,1)S(1)} %all_to_all.11.mine_ref, bf16[16,128,128]{2,1,0:T(8,128)(2,1)S(1)} %collective-permute-done.1.theirs_ref, f32[8,128,128]{2,1,0:T(8,128)S(1)} %copy-done.1), custom_call_target="tpu_custom_call" | custom-call | flops 268435456 | bytes 4194304 | tf_op jit(solution)/shard_map/pallas_call | solution.py:385
  78.5 0.5 collective-permute-start.2
  79.0 2.7 %shard_map.55.refs_0_ = bf16[1536,1024]{1,0:T(8,128)(2,1)} custom-call(bf16[1536,1024]{1,0:T(8,128)(2,1)S(1)} %get-tuple-element.13.x_ref, bf16[8,1536,128]{2,1,0:T(8,128)(2,1)S(1)} %get-tuple-element.14.v_ref, bf16[16,272,128]{2,1,0:T(8,128)(2,1)S(1)} %get-tuple-element.20.s_ref), custom_call_target="tpu_custom_call" | custom-call | flops 1610612736 | bytes 6291456 | tf_op jit(solution)/shard_map/pallas_call | solution.py:318
  81.6 0.0 collective-permute-done.2.s_ref
  81.6 3.2 %shard_map.56 = (bf16[1536,1024]{1,0:T(8,128)(2,1)}, f32[1,1024]{1,0:T(1,128)}) custom-call(bf16[1536,1024]{1,0:T(8,128)(2,1)S(1)} %get-tuple-element.13.x_ref, bf16[8,1536,128]{2,1,0:T(8,128)(2,1)S(1)} %get-tuple-element.14.v_ref, bf16[16,272,128]{2,1,0:T(8,128)(2,1)S(1)} %collective-permute-done.2.s_ref, ...), custom_call_target="tpu_custom_call", output_to_operand_aliasing={{0}: (3, {})} | custom-call | flops 1610612736 | bytes 6291456 | tf_op jit(solution)/shard_map/pallas_call | solution.py:318
  (1 shorter events, 0.0 us)
Async XLA Ops:
  8.7 4.8 %collective-permute-start = (bf16[16,400,128]{2,1,0:T(8,128)(2,1)}, bf16[16,400,128]{2,1,0:T(8,128)(2,1)S(1)}, u32[]{:S(2)}, u32[]{:S(2)}) collective-permute-start(bf16[16,400,128]{2,1,0:T(8,128)(2,1)} %get-tuple-element.19), channel_id=1, source_target_pairs={{0,4},{4,0},{1,5},{5,1},{2,6},{6,2},{3,7},{7,3},{8,12},{12,8},{9,1... | collective-permute-start | bytes 4915208 | tf_op jit(solution)/shard_map/ppermute | solution.py:334
  10.1 3.3 %copy-start = (bf16[16,128,128]{2,1,0:T(8,128)(2,1)S(1)}, bf16[16,128,128]{2,1,0:T(8,128)(2,1)}, u32[]{:S(2)}) copy-start(bf16[16,128,128]{2,1,0:T(8,128)(2,1)} %get-tuple-element.17.gram_ref) | copy-start | bytes 1572868
  10.1 3.3 %copy-start.2 = (f32[8,128]{1,0:T(8,128)S(1)}, f32[8,128]{1,0:T(8,128)}, u32[]{:S(2)}) copy-start(f32[8,128]{1,0:T(8,128)} %get-tuple-element.18.diag_ref) | copy-start | bytes 12292
  44.4 29.3 %copy-start.1 = (f32[8,128,128]{2,1,0:T(8,128)S(1)}, f32[8,128,128]{2,1,0:T(8,128)}, u32[]{:S(2)}) copy-start(f32[8,128,128]{2,1,0:T(8,128)} %t_ref.1) | copy-start | bytes 1572868
  69.3 4.5 %collective-permute-start.1 = (bf16[16,128,128]{2,1,0:T(8,128)(2,1)S(1)}, bf16[16,128,128]{2,1,0:T(8,128)(2,1)S(1)}, u32[]{:S(2)}, u32[]{:S(2)}) collective-permute-start(bf16[16,128,128]{2,1,0:T(8,128)(2,1)S(1)} %slice.4), channel_id=1, source_target_pairs={{0,4},{4,0},{1,5},{5,1},{2,6},{6,2},{3,7},{7,3},{8,12},{12,8},{9,1... | collective-permute-start | bytes 1572872 | tf_op jit(solution)/shard_map/ppermute | solution.py:334
  78.5 3.1 %collective-permute-start.2 = (bf16[16,272,128]{2,1,0:T(8,128)(2,1)S(1)}, bf16[16,272,128]{2,1,0:T(8,128)(2,1)S(1)}, u32[]{:S(2)}, u32[]{:S(2)}) collective-permute-start(bf16[16,272,128]{2,1,0:T(8,128)(2,1)S(1)} %get-tuple-element.20.s_ref), channel_id=1, source_target_pairs={{0,4},{4,0},{1,5},{5,1},{2,6},{6,2},{3,7},{7,3},{8,12},{12,8},{9,1... | collective-permute-start | bytes 3342344 | tf_op jit(solution)/shard_map/ppermute | solution.py:334

commit v5 on v4

v5 whole, which is shorter than its diff:
```python
import functools

import jax
import jax.numpy as jnp
from jax import lax
from jax.experimental import pallas as pl
from jax.experimental.pallas import tpu as pltpu
from jax.sharding import PartitionSpec as P

NORD = 49152
WIDTH = 128
PANELS = 8
CHIPS = 16
OWN = 32
HALF = CHIPS * OWN
PAIRS = PANELS * (PANELS - 1) // 2
BLOCKS = PAIRS + PANELS // 2
SHARE = BLOCKS * WIDTH // (2 * CHIPS)
PROJ = PANELS * OWN
MORE = PROJ + SHARE
TILE = 16
CHUNK = MORE + TILE
STEP = 256
AHEAD = 2
BF = jnp.bfloat16
F32 = jnp.float32
SIDE = 4


def device(x, z, core):
    return (x * SIDE + z) * 2 + core


def lines(along_z):
    along_x = [[device(x, z, 1 - along_z) for x in range(SIDE)] for z in range(SIDE)]
    return [[device(x, z, along_z) for z in range(SIDE)] for x in range(SIDE)] + along_x


WIDE, NARROW = lines(0), lines(1)
VMEM = pl.BlockSpec(memory_space=pltpu.VMEM)
HBM = pl.BlockSpec(memory_space=pltpu.HBM)


def call(kernel, out_shape, in_specs, out_specs, flops, nbytes, limit=12, **kw):
    return pl.pallas_call(
        kernel,
        out_shape=out_shape,
        in_specs=in_specs,
        out_specs=out_specs,
        compiler_params=pltpu.CompilerParams(vmem_limit_bytes=limit * 2**20),
        cost_estimate=pl.CostEstimate(flops=flops, bytes_accessed=nbytes, transcendentals=0),
        **kw,
    )


def core_index():
    return lax.rem(lax.axis_index("row"), 2)


def first_block(k):
    return k * (k - 1) // 2


def load(source, target, sem):
    copy = pltpu.make_async_copy(source, target, sem)
    copy.start()
    return copy


def pair(v_ref, k):
    return jnp.concatenate([v_ref[k], v_ref[k + 1]], axis=1)


def parts_of(value):
    parts = []
    for _ in range(3):
        part = value.astype(BF).astype(F32)
        parts.append(part)
        value = value - part
    return parts


def packed(values):
    row = lax.broadcasted_iota(jnp.int32, (TILE, WIDTH), 0)
    tile = jnp.zeros((TILE, WIDTH), F32)
    for i, value in enumerate(values):
        for j, part in enumerate(parts_of(value)):
            tile = jnp.where(row == 3 * i + j, part, tile)
    return tile.astype(BF)


def unpacked(tile, count):
    tile = tile.astype(F32)
    return [
        tile[3 * i : 3 * i + 1] + tile[3 * i + 1 : 3 * i + 2] + tile[3 * i + 2 : 3 * i + 3]
        for i in range(count)
    ]


def squares_of(x):
    wide = x.astype(F32)
    return jnp.sum(wide * wide, axis=0, keepdims=True)


def put(p_ref, n, k, both):
    chips = slice(n // OWN, (n + STEP) // OWN)
    for dk in range(2):
        p_ref[chips, (k + dk) * OWN : (k + dk + 1) * OWN, :] = (
            both[:, dk * WIDTH : (dk + 1) * WIDTH].astype(BF).reshape(STEP // OWN, OWN, WIDTH)
        )


def project(x_ref, v_ref, half, p_ref):
    squares = []
    for n in range(0, HALF, STEP):
        x = x_ref[:, pl.ds(pl.multiple_of(half * HALF + n, STEP), STEP)]
        squares.append(squares_of(x))
        xt = x.T
        for k in range(0, PANELS, 2):
            put(p_ref, n, k, jnp.dot(xt, pair(v_ref, k), preferred_element_type=F32))
    return jnp.concatenate(squares, axis=1)


def group_of(values, s):
    at = s * OWN // WIDTH * WIDTH
    return values[:, at : at + WIDTH]


def first_kernel(
    x_hbm, v_hbm, other_ref, mine_ref, diag_ref, x_ref, v_ref, xt_ref, vt_ref, sems
):
    core = core_index()
    half = 1 - core

    def columns(half, n):
        return pl.ds(pl.multiple_of(half * HALF + n * STEP, STEP), STEP)

    def of_x(half, n):
        at = columns(half, n)
        return x_hbm.at[:, at], x_ref.at[:, at]

    def of_v(k):
        return v_hbm.at[2 * k : 2 * k + 2], v_ref.at[2 * k : 2 * k + 2]

    queue = [of_x(half, 0), of_v(0), of_v(1), of_x(half, 1), of_v(2), of_v(3)]
    queue += [of_x(core, 0), of_x(core, 1)]
    copies = []

    def start():
        if len(copies) < len(queue):
            copies.append(load(*queue[len(copies)], sems.at[len(copies)]))

    def arrived(i):
        copies[i].wait()
        start()

    for _ in range(AHEAD):
        start()
    row = lax.broadcasted_iota(jnp.int32, (WIDTH, WIDTH), 0)
    column = lax.broadcasted_iota(jnp.int32, (WIDTH, WIDTH), 1)
    squares = [None] * (HALF // STEP)
    diag = []

    def turn(n):
        x = x_ref[:, columns(half, n)]
        xt_ref[n] = x.T
        squares[n] = squares_of(x)

    def product(n, k):
        put(
            other_ref,
            n * STEP,
            2 * k,
            jnp.dot(xt_ref[n], pair(v_ref, 2 * k), preferred_element_type=F32),
        )

    def keep(block, value):
        sent = core != block // CHIPS
        value = value.astype(BF)
        spot = block % CHIPS
        other_ref[jnp.where(sent, spot, CHIPS), PROJ:MORE, :] = value
        mine_ref[jnp.where(sent, CHIPS, spot)] = value

    def gram(j, k):
        both = jnp.dot(vt_ref[j], pair(v_ref, 2 * k), preferred_element_type=F32)
        blocks = [
            [both[d * WIDTH : (d + 1) * WIDTH, e * WIDTH : (e + 1) * WIDTH] for e in range(2)]
            for d in range(2)
        ]
        for d in range(2):
            for e in range(2):
                if 2 * j + d < 2 * k + e:
                    keep(first_block(2 * k + e) + 2 * j + d, blocks[d][e])
        if j == k:
            keep(PAIRS + k, jnp.where(row < column, blocks[0][0], blocks[1][1]))
            for d in range(2):
                own = jnp.where(row == column, blocks[d][d], 0.0)
                diag.append(jnp.sum(own, axis=0, keepdims=True))

    def panels(k, tiles):
        vt_ref[k] = pair(v_ref, 2 * k).T
        for n in tiles:
            product(n, k)
        for j in range(k + 1):
            gram(j, k)

    arrived(0)
    turn(0)
    arrived(1)
    panels(0, [0])
    arrived(2)
    panels(1, [0])
    arrived(3)
    turn(1)
    product(1, 0)
    product(1, 1)
    arrived(4)
    panels(2, [0, 1])
    arrived(5)
    panels(3, [0, 1])
    squares = jnp.concatenate(squares, axis=1)
    for k in range(PANELS):
        diag_ref[k : k + 1, :] = diag[k]
    for s in range(CHIPS):
        other_ref[s, MORE:, :] = packed([group_of(squares, s), diag[s % PANELS]])
    arrived(6)
    arrived(7)


def own_kernel(x_ref, v_ref, p_ref, sq_ref):
    sq_ref[...] = project(x_ref, v_ref, core_index(), p_ref)


def combine_kernel(own_ref, sq_ref, gram_ref, diag_ref, other_ref, out_ref):
    for s in range(CHIPS):
        out_ref[s, :PROJ, :] = (
            own_ref[s].astype(F32) + other_ref[s, :PROJ, :].astype(F32)
        ).astype(BF)
        out_ref[s, PROJ:MORE, :] = (
            gram_ref[s].astype(F32) + other_ref[s, PROJ:MORE, :].astype(F32)
        ).astype(BF)
        squares, diag = unpacked(other_ref[s, MORE:, :], 2)
        k = s % PANELS
        out_ref[s, MORE:, :] = packed(
            [group_of(sq_ref[...], s) + squares, diag_ref[k : k + 1, :] + diag]
        )


def sum_kernel(parts_ref, out_ref):
    senders, rows = parts_ref.shape[:2]
    chunks = rows // CHUNK
    for i in range(chunks):
        for at in range(0, CHUNK, TILE):
            here = slice(i * CHUNK + at, i * CHUNK + at + TILE)
            total = parts_ref[0, here, :].astype(F32)
            for s in range(1, senders):
                total = total + parts_ref[s, here, :].astype(F32)
            total = packed(unpacked(total, 2)) if at == MORE else total.astype(BF)
            for s in range(i, SIDE, chunks):
                out_ref[s, at : at + TILE, :] = total


def spread_kernel(chunks_ref, out_ref):
    for j in range(SIDE):
        for i in range(SIDE):
            out_ref[j, i * CHUNK : (i + 1) * CHUNK, :] = chunks_ref[i]


def split(value):
    high = value.astype(BF)
    return high, (value - high.astype(F32)).astype(BF)


def solve_kernel(mine_ref, theirs_ref, t_ref, out_ref, dev_ref, g_ref):
    core = core_index()
    for s in range(CHIPS):
        at = pl.multiple_of(core * CHIPS * SHARE + s * SHARE, 16)
        g_ref[pl.ds(at, SHARE), :] = mine_ref[s, PROJ:MORE, :]
        at = pl.multiple_of((1 - core) * CHIPS * SHARE + s * SHARE, 16)
        g_ref[pl.ds(at, SHARE), :] = theirs_ref[s]
    row = lax.broadcasted_iota(jnp.int32, (WIDTH, WIDTH), 0)
    column = lax.broadcasted_iota(jnp.int32, (WIDTH, WIDTH), 1)
    done = []
    change = jnp.zeros((HALF, WIDTH), F32)
    for k in range(PANELS + 1):
        rows = slice(k * OWN, (k + 1) * OWN)
        if k:
            at = (PAIRS + (k - 1) // 2) * WIDTH
            own = g_ref[at : at + WIDTH, :].astype(F32)
            own = jnp.where(row < column if k % 2 else row > column, 2.0 * own, 0.0).astype(BF)
            if k > 1:
                own = jnp.concatenate([jnp.zeros(((k - 1) * WIDTH, WIDTH), BF), own], axis=0)
            right = own
            if k < PANELS:
                at = first_block(k) * WIDTH
                right = jnp.concatenate([g_ref[at : at + k * WIDTH, :], own], axis=1)
            else:
                right, done = own[-WIDTH:], done[-1:]
            before = jnp.concatenate(done, axis=1) if len(done) > 1 else done[0]
            both = jnp.dot(before, right, preferred_element_type=F32)
            change += done[-1].astype(F32) * both[:, -WIDTH:]
        if k == PANELS:
            break
        proj = mine_ref[:, rows, :].reshape(HALF, WIDTH).astype(F32)
        if k:
            proj = proj - both[:, :WIDTH]
        factor, rest = split(t_ref[k])
        high, low = split(proj)
        scaled = lax.dot_general(
            jnp.concatenate([high, low, high], axis=1),
            jnp.concatenate([factor, factor, rest], axis=1),
            (((1,), (1,)), ((), ())),
            preferred_element_type=F32,
        ).astype(BF)
        done.append(scaled)
        out_ref[:, rows, :] = scaled.reshape(CHIPS, OWN, WIDTH)
        wide = scaled.astype(F32)
        change += wide * (wide * unpacked(mine_ref[k, MORE:, :], 2)[1] - 2.0 * proj)
    squares = jnp.sum(change.T, axis=0, keepdims=True)
    before = jnp.concatenate(
        [
            unpacked(mine_ref[s, MORE:, :], 2)[0]
            for s in range(0, CHIPS, WIDTH // OWN)
        ],
        axis=1,
    )
    deviation = jnp.sqrt(jnp.maximum(before + squares, 0.0) / NORD) - 1.0
    dev_ref[...] = deviation
    tile = packed([deviation[:, n : n + WIDTH] for n in range(0, HALF, WIDTH)])
    for s in range(CHIPS):
        out_ref[s, PROJ:, :] = tile


def update_kernel(flip, x_ref, v_ref, s_ref, *refs):
    out_hbm, *more, out_ref, sems = refs[2:] if flip else refs
    core = core_index()
    half = 1 - core if flip else core
    left = jnp.concatenate([v_ref[k] for k in range(PANELS)], axis=1)
    stores = []
    for n in range(0, HALF, STEP):
        chips = slice(n // OWN, (n + STEP) // OWN)
        right = jnp.concatenate(
            [s_ref[chips, k * OWN : (k + 1) * OWN, :].reshape(STEP, WIDTH) for k in range(PANELS)],
            axis=1,
        )
        update = lax.dot_general(left, right, (((1,), (1,)), ((), ())), preferred_element_type=F32)
        columns = pl.ds(pl.multiple_of(half * HALF + n, STEP), STEP)
        i = n // STEP
        out_ref[i] = (x_ref[:, columns].astype(F32) - update).astype(BF)
        stores.append(load(out_ref.at[i], out_hbm.at[:, columns], sems.at[i]))
    if flip:
        theirs = jnp.concatenate(unpacked(s_ref[0, PROJ:, :], HALF // WIDTH), axis=1)
        more[0][:, pl.ds(pl.multiple_of(core * HALF, HALF), HALF)] = refs[1][...]
        more[0][:, pl.ds(pl.multiple_of(half * HALF, HALF), HALF)] = theirs
    for store in stores:
        store.wait()


def update(flip, eigvecs, reflectors, scaled, *so_far):
    rows = eigvecs.shape[0]
    tiles = HALF // STEP
    in_specs = [VMEM] * 3
    out_shape = jax.ShapeDtypeStruct(eigvecs.shape, BF)
    out_specs = HBM
    aliases = {}
    if flip:
        in_specs += [HBM, VMEM]
        aliases = {3: 0}
        out_shape = (out_shape, jax.ShapeDtypeStruct((1, 2 * HALF), F32))
        out_specs = (HBM, VMEM)
    return call(
        functools.partial(update_kernel, flip),
        out_shape,
        in_specs,
        out_specs,
        2 * rows * HALF * PANELS * WIDTH,
        6 * 2**20,
        input_output_aliases=aliases,
        scratch_shapes=[
            pltpu.VMEM((tiles, rows, STEP), BF),
            pltpu.SemaphoreType.DMA((tiles,)),
        ],
    )(eigvecs, reflectors, scaled, *so_far)


def swapped(value):
    pairs = [(i ^ 1, i) for i in range(2 * CHIPS)]
    return lax.ppermute(value, "row", pairs)


def exchanged(value, groups):
    return lax.all_to_all(
        value, "row", split_axis=0, concat_axis=0, axis_index_groups=groups, tiled=True
    )


def steps(eigvecs, reflectors, factors):
    rows = eigvecs.shape[0]
    flops = 2 * rows * HALF * PANELS * WIDTH
    chunks = jax.ShapeDtypeStruct((CHIPS, CHUNK, WIDTH), BF)
    tiles = HALF // STEP
    other, gram, diag, eigvecs, reflectors = call(
        first_kernel,
        (
            jax.ShapeDtypeStruct((CHIPS + 1, CHUNK, WIDTH), BF),
            jax.ShapeDtypeStruct((CHIPS + 1, SHARE, WIDTH), BF),
            jax.ShapeDtypeStruct((PANELS, WIDTH), F32),
            pltpu.VMEM(eigvecs.shape, BF),
            pltpu.VMEM(reflectors.shape, BF),
        ),
        [HBM] * 2,
        (VMEM,) * 5,
        2 * flops,
        8 * 2**20,
        limit=54,
        scratch_shapes=[
            pltpu.VMEM((tiles, STEP, rows), BF),
            pltpu.VMEM((PANELS // 2, 2 * WIDTH, rows), BF),
            pltpu.SemaphoreType.DMA((2 * tiles + PANELS // 2,)),
        ],
    )(eigvecs, reflectors)
    other = swapped(other)
    own, squares = call(
        own_kernel,
        (
            jax.ShapeDtypeStruct((CHIPS, PROJ, WIDTH), BF),
            jax.ShapeDtypeStruct((1, HALF), F32),
        ),
        [VMEM] * 2,
        (VMEM,) * 2,
        flops,
        6 * 2**20,
    )(eigvecs, reflectors)
    payload = call(combine_kernel, chunks, [VMEM] * 5, VMEM, 2**20, 4 * 2**20)(
        own, squares, gram, diag, other
    )
    lot = jax.ShapeDtypeStruct((SIDE, CHUNK, WIDTH), BF)
    lots = jax.ShapeDtypeStruct((SIDE, SIDE * CHUNK, WIDTH), BF)
    for groups in (WIDE, NARROW):
        parts = exchanged(payload.reshape(SIDE, -1, WIDTH), groups)
        payload = call(sum_kernel, lot, [VMEM], VMEM, 2**20, 2 * 2**20)(parts)
    gathered = exchanged(payload, NARROW)
    gathered = call(spread_kernel, lots, [VMEM], VMEM, 2**20, 2 * 2**20)(gathered)
    mine = exchanged(gathered, WIDE).reshape(CHIPS, CHUNK, WIDTH)
    theirs = swapped(mine[:, PROJ:MORE, :])
    scaled, dev = call(
        solve_kernel,
        (
            jax.ShapeDtypeStruct((CHIPS, PROJ + TILE, WIDTH), BF),
            jax.ShapeDtypeStruct((1, HALF), F32),
        ),
        [VMEM] * 3,
        (VMEM,) * 2,
        2**28,
        4 * 2**20,
        scratch_shapes=[pltpu.VMEM((BLOCKS * WIDTH, WIDTH), BF)],
    )(mine, theirs, factors)
    scaled_theirs = swapped(scaled)
    vectors = update(False, eigvecs, reflectors, scaled)
    vectors, deviation = update(True, eigvecs, reflectors, scaled_theirs, vectors, dev)
    return (vectors, deviation.reshape(-1))


def solution(mesh):
    placed = (P("row", "col"), P(None, "row", None), P())
    return jax.shard_map(
        steps, mesh=mesh, in_specs=placed, out_specs=(P("row", "col"), P("col")), check_vma=False
    )
```

time: 85.1 us -> 86.6 us (1.018)
  blocking collectives: 55 us -> 52.4 us
  starting transfers between devices: 4.84 us -> 7.38 us
  Pallas kernels: 21.3 us -> 22.4 us
    all_to_all x2 -> x4, blocking collectives: 55 us -> 52.4 us  [exchanged(): lax.all_to_all(value, 'row', split_axis=0, concat_axis=0, axis_index_grou...]
    ppermute x3, starting transfers between devices: 4.84 us -> 7.38 us  [swapped(): return lax.ppermute(value, 'row', pairs)]
    pallas_call x2 -> x4, Pallas kernels: 8.28 us -> 9.42 us  [the longest x1 8.91 us: steps(): call(first_kernel, (jax.ShapeDtypeStruct((CHIPS + 1, CHUNK, WIDTH), BF),...]
  transfers between devices with their start and end apart: 3 -> 3, of which waited for: 2 -> 2; matrix products, arithmetic and copies ran while one was open for 0% -> 0% of each run, Pallas kernels for 5% -> 6%
where the time goes in v5:
time: 86.6 us; the launch traced here: 86.3 us
  blocking collectives  52.4 us (61%)
  Pallas kernels  22.4 us (26%)
  starting transfers between devices  7.38 us (9%)
  waiting for transfers between devices  3.17 us (4%)
    all_to_all x4, blocking collectives, exchanged(): lax.all_to_all(value, 'row', split_axis=0, concat_axis=0, axis_index_grou...  52.4 us
    pallas_call x1, Pallas kernels, steps(): call(first_kernel, (jax.ShapeDtypeStruct((CHIPS + 1, CHUNK, WIDTH), BF),...  8.91 us
    ppermute x3, starting transfers between devices, swapped(): return lax.ppermute(value, 'row', pairs)  7.38 us
    pallas_call x2, Pallas kernels, update(): call(functools.partial(update_kernel, flip), out_shape, in_specs, out_spe...  6.65 us
    pallas_call x1, Pallas kernels, steps(): call(solve_kernel, (jax.ShapeDtypeStruct((CHIPS, PROJ + TILE, WIDTH), BF)...  4.01 us
    ppermute x3, waiting for transfers between devices, swapped(): return lax.ppermute(value, 'row', pairs)  3.17 us
    pallas_call x1, Pallas kernels, steps(): call(own_kernel, (jax.ShapeDtypeStruct((CHIPS, PROJ, WIDTH), BF), jax.Sha...  1.85 us
  transfers between devices with their start and end apart: 3, of which 2 were waited for; matrix products, arithmetic and copies ran while one was open for 0% of the time, Pallas kernels for 6%

profile of v5, /device:TPU:1, one launch (start us, length us, event | category | flops | bytes accessed | tf_op | source)
XLA Modules:
  0.0 86.3 jit_solution(5728458527913554589)
XLA Ops:
  0.6 8.9 %shard_map.50 = (bf16[17,400,128]{2,1,0:T(8,128)(2,1)}, bf16[17,128,128]{2,1,0:T(8,128)(2,1)}, f32[8,128]{1,0:T(8,128)}, bf16[1536,1024]{1,0:T(8,128)(2,1)S(1)}, bf16[8,1536,128]{2,1,0:T(8,128)(2,1)S(1)}) custom-call(bf16[1536,1024]{1,0:T(8,128)(2,1)} %x_hbm.1, bf16[8,1536,128]{2,1,0:T(8,128)(2,1)} %v_hbm.1), custom_call_target="tpu_custom_call" | custom-call | flops 3221225472 | bytes 8388608 | tf_op jit(solution)/shard_map/pallas_call | solution.py:402
  9.6 1.4 %collective-permute-start = (bf16[17,400,128]{2,1,0:T(8,128)(2,1)}, bf16[17,400,128]{2,1,0:T(8,128)(2,1)S(1)}, u32[]{:S(2)}, u32[]{:S(2)}) collective-permute-start(bf16[17,400,128]{2,1,0:T(8,128)(2,1)} %get-tuple-element.19), channel_id=1, source_target_pairs={{4,0},{0,4},{12,8},{8,12},{20,16},{16,20},{28,24},{24,28},{36,32},... | collective-permute-start | bytes 5222408 | tf_op jit(solution)/shard_map/ppermute | solution.py:388
  11.0 0.0 copy-start
  11.0 1.8 %shard_map.51 = (bf16[16,256,128]{2,1,0:T(8,128)(2,1)S(1)}, f32[1,512]{1,0:T(1,128)S(1)}) custom-call(bf16[1536,1024]{1,0:T(8,128)(2,1)S(1)} %get-tuple-element.13.x_ref, bf16[8,1536,128]{2,1,0:T(8,128)(2,1)S(1)} %get-tuple-element.14.v_ref), custom_call_target="tpu_custom_call" | custom-call | flops 1610612736 | bytes 6291456 | tf_op jit(solution)/shard_map/pallas_call | solution.py:423
  12.9 1.6 %collective-permute-done.other_ref = bf16[17,400,128]{2,1,0:T(8,128)(2,1)S(1)} collective-permute-done((bf16[17,400,128]{2,1,0:T(8,128)(2,1)}, bf16[17,400,128]{2,1,0:T(8,128)(2,1)S(1)}, u32[]{:S(2)}, u32[]{:S(2)}) %collective-permute-start) | collective-permute-done | bytes 1740832 | tf_op jit(solution)/shard_map/ppermute | solution.py:388
  14.5 0.0 copy-done
  14.5 0.0 copy-done.2
  14.5 0.5 shard_map.52
  15.0 16.8 %all_to_all.20.parts_ref = bf16[4,1600,128]{2,1,0:T(8,128)(2,1)S(1)} all-to-all(bf16[4,1600,128]{2,1,0:T(8,128)(2,1)S(1)} %bitcast.5), channel_id=1, replica_groups={{0,8,16,24},{32,40,48,56},{64,72,80,88},{96,104,112,120},{4,36,68,100},..., dimensions={0} | all-to-all | bytes 3276800 | tf_op jit(solution)/shard_map/all_to_all | solution.py:392
  31.8 0.2 shard_map.53
  32.0 11.1 %all_to_all.21.parts_ref = bf16[4,400,128]{2,1,0:T(8,128)(2,1)S(1)} all-to-all(bf16[4,400,128]{2,1,0:T(8,128)(2,1)S(1)} %shard_map.53), channel_id=1, replica_groups={{4,12,20,28},{36,44,52,60},{68,76,84,92},{100,108,116,124},{0,32,64,96}..., dimensions={0} | all-to-all | bytes 819200 | tf_op jit(solution)/shard_map/all_to_all | solution.py:392
  43.1 0.1 shard_map.54
  43.2 8.7 %all_to_all.22.chunks_ref = bf16[4,400,128]{2,1,0:T(8,128)(2,1)S(1)} all-to-all(bf16[4,400,128]{2,1,0:T(8,128)(2,1)S(1)} %shard_map.54), channel_id=1, replica_groups={{4,12,20,28},{36,44,52,60},{68,76,84,92},{100,108,116,124},{0,32,64,96}..., dimensions={0} | all-to-all | bytes 819200 | tf_op jit(solution)/shard_map/all_to_all | solution.py:392
  51.9 0.2 shard_map.55
  52.1 0.0 copy-start.1
  52.1 15.8 %all_to_all.23 = bf16[4,1600,128]{2,1,0:T(8,128)(2,1)S(1)} all-to-all(bf16[4,1600,128]{2,1,0:T(8,128)(2,1)S(1)} %shard_map.55), channel_id=1, replica_groups={{0,8,16,24},{32,40,48,56},{64,72,80,88},{96,104,112,120},{4,36,68,100},..., dimensions={0} | all-to-all | bytes 3276800 | tf_op jit(solution)/shard_map/all_to_all | solution.py:392
  67.9 5.3 %collective-permute-start.1 = (bf16[16,128,128]{2,1,0:T(8,128)(2,1)S(1)}, bf16[16,128,128]{2,1,0:T(8,128)(2,1)S(1)}, u32[]{:S(2)}, u32[]{:S(2)}) collective-permute-start(bf16[16,128,128]{2,1,0:T(8,128)(2,1)S(1)} %slice.4), channel_id=1, source_target_pairs={{4,0},{0,4},{12,8},{8,12},{20,16},{16,20},{28,24},{24,28},{36,32},... | collective-permute-start | bytes 1572872 | tf_op jit(solution)/shard_map/ppermute | solution.py:388
  73.2 1.5 %collective-permute-done.1.theirs_ref = bf16[16,128,128]{2,1,0:T(8,128)(2,1)S(1)} collective-permute-done((bf16[16,128,128]{2,1,0:T(8,128)(2,1)S(1)}, bf16[16,128,128]{2,1,0:T(8,128)(2,1)S(1)}, u32[]{:S(2)}, u32[]{:S(2)}) %collective-permute-start.1) | collective-permute-done | bytes 524320 | tf_op jit(solution)/shard_map/ppermute | solution.py:388
  74.8 0.0 copy-done.1
  74.8 4.0 %shard_map.56 = (bf16[16,272,128]{2,1,0:T(8,128)(2,1)S(1)}, f32[1,512]{1,0:T(1,128)S(1)}) custom-call(bf16[16,400,128]{2,1,0:T(8,128)(2,1)S(1)} %bitcast.4, bf16[16,128,128]{2,1,0:T(8,128)(2,1)S(1)} %collective-permute-done.1.theirs_ref, f32[8,128,128]{2,1,0:T(8,128)S(1)} %copy-done.1), custom_call_target="tpu_custom_call" | custom-call | flops 268435456 | bytes 4194304 | tf_op jit(solution)/shard_map/pallas_call | solution.py:446
  78.8 0.6 collective-permute-start.2
  79.4 3.0 %shard_map.57.refs_0_ = bf16[1536,1024]{1,0:T(8,128)(2,1)} custom-call(bf16[1536,1024]{1,0:T(8,128)(2,1)S(1)} %get-tuple-element.13.x_ref, bf16[8,1536,128]{2,1,0:T(8,128)(2,1)S(1)} %get-tuple-element.14.v_ref, bf16[16,272,128]{2,1,0:T(8,128)(2,1)S(1)} %get-tuple-element.20.s_ref), custom_call_target="tpu_custom_call" | custom-call | flops 1610612736 | bytes 6291456 | tf_op jit(solution)/shard_map/pallas_call | solution.py:371
  82.5 0.0 collective-permute-done.2.s_ref
  82.5 3.6 %shard_map.58 = (bf16[1536,1024]{1,0:T(8,128)(2,1)}, f32[1,1024]{1,0:T(1,128)}) custom-call(bf16[1536,1024]{1,0:T(8,128)(2,1)S(1)} %get-tuple-element.13.x_ref, bf16[8,1536,128]{2,1,0:T(8,128)(2,1)S(1)} %get-tuple-element.14.v_ref, bf16[16,272,128]{2,1,0:T(8,128)(2,1)S(1)} %collective-permute-done.2.s_ref, ...), custom_call_target="tpu_custom_call", output_to_operand_aliasing={{0}: (3, {})} | custom-call | flops 1610612736 | bytes 6291456 | tf_op jit(solution)/shard_map/pallas_call | solution.py:371
  (2 shorter events, 0.0 us)
Async XLA Ops:
  9.6 4.9 %collective-permute-start = (bf16[17,400,128]{2,1,0:T(8,128)(2,1)}, bf16[17,400,128]{2,1,0:T(8,128)(2,1)S(1)}, u32[]{:S(2)}, u32[]{:S(2)}) collective-permute-start(bf16[17,400,128]{2,1,0:T(8,128)(2,1)} %get-tuple-element.19), channel_id=1, source_target_pairs={{4,0},{0,4},{12,8},{8,12},{20,16},{16,20},{28,24},{24,28},{36,32},... | collective-permute-start | bytes 5222408 | tf_op jit(solution)/shard_map/ppermute | solution.py:388
  11.0 3.5 %copy-start = (bf16[17,128,128]{2,1,0:T(8,128)(2,1)S(1)}, bf16[17,128,128]{2,1,0:T(8,128)(2,1)}, u32[]{:S(2)}) copy-start(bf16[17,128,128]{2,1,0:T(8,128)(2,1)} %get-tuple-element.17.gram_ref) | copy-start | bytes 1671172
  11.0 3.5 %copy-start.2 = (f32[8,128]{1,0:T(8,128)S(1)}, f32[8,128]{1,0:T(8,128)}, u32[]{:S(2)}) copy-start(f32[8,128]{1,0:T(8,128)} %get-tuple-element.18.diag_ref) | copy-start | bytes 12292
  52.1 22.7 %copy-start.1 = (f32[8,128,128]{2,1,0:T(8,128)S(1)}, f32[8,128,128]{2,1,0:T(8,128)}, u32[]{:S(2)}) copy-start(f32[8,128,128]{2,1,0:T(8,128)} %t_ref.1) | copy-start | bytes 1572868
  67.9 6.9 %collective-permute-start.1 = (bf16[16,128,128]{2,1,0:T(8,128)(2,1)S(1)}, bf16[16,128,128]{2,1,0:T(8,128)(2,1)S(1)}, u32[]{:S(2)}, u32[]{:S(2)}) collective-permute-start(bf16[16,128,128]{2,1,0:T(8,128)(2,1)S(1)} %slice.4), channel_id=1, source_target_pairs={{4,0},{0,4},{12,8},{8,12},{20,16},{16,20},{28,24},{24,28},{36,32},... | collective-permute-start | bytes 1572872 | tf_op jit(solution)/shard_map/ppermute | solution.py:388
  78.8 3.7 %collective-permute-start.2 = (bf16[16,272,128]{2,1,0:T(8,128)(2,1)S(1)}, bf16[16,272,128]{2,1,0:T(8,128)(2,1)S(1)}, u32[]{:S(2)}, u32[]{:S(2)}) collective-permute-start(bf16[16,272,128]{2,1,0:T(8,128)(2,1)S(1)} %get-tuple-element.20.s_ref), channel_id=1, source_target_pairs={{4,0},{0,4},{12,8},{8,12},{20,16},{16,20},{28,24},{24,28},{36,32},... | collective-permute-start | bytes 3342344 | tf_op jit(solution)/shard_map/ppermute | solution.py:388

commit v6 on v5

--- a/solution.py
+++ b/solution.py
@@ -21,7 +21,7 @@
 TILE = 16
 CHUNK = MORE + TILE
 STEP = 256
-AHEAD = 2
+AHEAD = 5
 BF = jnp.bfloat16
 F32 = jnp.float32
 SIDE = 4
@@ -36,7 +36,14 @@
     return [[device(x, z, along_z) for z in range(SIDE)] for x in range(SIDE)] + along_x
 
 
-WIDE, NARROW = lines(0), lines(1)
+LINES = lines(0)
+
+
+def swap_pairs(partner):
+    return [(line[i], line[partner(i)]) for line in lines(1) for i in range(SIDE)]
+
+
+SWAPS = (swap_pairs(lambda i: i ^ 1), swap_pairs(lambda i: SIDE - 1 - i))
 VMEM = pl.BlockSpec(memory_space=pltpu.VMEM)
 HBM = pl.BlockSpec(memory_space=pltpu.HBM)
 
@@ -246,24 +253,31 @@
         )
 
 
+def sum_tiles(parts, at):
+    total = parts[0].astype(F32)
+    for part in parts[1:]:
+        total = total + part.astype(F32)
+    return packed(unpacked(total, 2)) if at == MORE else total.astype(BF)
+
+
 def sum_kernel(parts_ref, out_ref):
-    senders, rows = parts_ref.shape[:2]
-    chunks = rows // CHUNK
-    for i in range(chunks):
+    for i in range(SIDE):
         for at in range(0, CHUNK, TILE):
             here = slice(i * CHUNK + at, i * CHUNK + at + TILE)
-            total = parts_ref[0, here, :].astype(F32)
-            for s in range(1, senders):
-                total = total + parts_ref[s, here, :].astype(F32)
-            total = packed(unpacked(total, 2)) if at == MORE else total.astype(BF)
-            for s in range(i, SIDE, chunks):
-                out_ref[s, at : at + TILE, :] = total
-
-
-def spread_kernel(chunks_ref, out_ref):
-    for j in range(SIDE):
-        for i in range(SIDE):
-            out_ref[j, i * CHUNK : (i + 1) * CHUNK, :] = chunks_ref[i]
+            parts = [parts_ref[s, here, :] for s in range(SIDE)]
+            out_ref[i, at : at + TILE, :] = sum_tiles(parts, at)
+
+
+def add_kernel(mine_ref, theirs_ref, out_ref):
+    for i in range(SIDE):
+        for at in range(0, CHUNK, TILE):
+            here = slice(at, at + TILE)
+            total = sum_tiles([mine_ref[i, here, :], theirs_ref[i, here, :]], at)
+            if out_ref.shape[1] == CHUNK:
+                out_ref[i, here, :] = total
+            else:
+                for j in range(SIDE):
+                    out_ref[j, i * CHUNK + at : i * CHUNK + at + TILE, :] = total
 
 
 def split(value):
@@ -332,11 +346,10 @@
 
 
 def update_kernel(flip, x_ref, v_ref, s_ref, *refs):
-    out_hbm, *more, out_ref, sems = refs[2:] if flip else refs
+    out_hbm, *more, out_ref, sem = refs[2:] if flip else refs
     core = core_index()
     half = 1 - core if flip else core
     left = jnp.concatenate([v_ref[k] for k in range(PANELS)], axis=1)
-    stores = []
     for n in range(0, HALF, STEP):
         chips = slice(n // OWN, (n + STEP) // OWN)
         right = jnp.concatenate(
@@ -345,20 +358,18 @@
         )
         update = lax.dot_general(left, right, (((1,), (1,)), ((), ())), preferred_element_type=F32)
         columns = pl.ds(pl.multiple_of(half * HALF + n, STEP), STEP)
-        i = n // STEP
-        out_ref[i] = (x_ref[:, columns].astype(F32) - update).astype(BF)
-        stores.append(load(out_ref.at[i], out_hbm.at[:, columns], sems.at[i]))
+        out_ref[:, n : n + STEP] = (x_ref[:, columns].astype(F32) - update).astype(BF)
+    columns = pl.ds(pl.multiple_of(half * HALF, HALF), HALF)
+    store = load(out_ref, out_hbm.at[:, columns], sem)
     if flip:
         theirs = jnp.concatenate(unpacked(s_ref[0, PROJ:, :], HALF // WIDTH), axis=1)
         more[0][:, pl.ds(pl.multiple_of(core * HALF, HALF), HALF)] = refs[1][...]
         more[0][:, pl.ds(pl.multiple_of(half * HALF, HALF), HALF)] = theirs
-    for store in stores:
-        store.wait()
+    store.wait()
 
 
 def update(flip, eigvecs, reflectors, scaled, *so_far):
     rows = eigvecs.shape[0]
-    tiles = HALF // STEP
     in_specs = [VMEM] * 3
     out_shape = jax.ShapeDtypeStruct(eigvecs.shape, BF)
     out_specs = HBM
@@ -377,20 +388,22 @@
         6 * 2**20,
         input_output_aliases=aliases,
         scratch_shapes=[
-            pltpu.VMEM((tiles, rows, STEP), BF),
-            pltpu.SemaphoreType.DMA((tiles,)),
+            pltpu.VMEM((rows, HALF), BF),
+            pltpu.SemaphoreType.DMA,
         ],
     )(eigvecs, reflectors, scaled, *so_far)
 
 
-def swapped(value):
-    pairs = [(i ^ 1, i) for i in range(2 * CHIPS)]
+CORES = [(i ^ 1, i) for i in range(2 * CHIPS)]
+
+
+def swapped(value, pairs=CORES):
     return lax.ppermute(value, "row", pairs)
 
 
-def exchanged(value, groups):
+def exchanged(value):
     return lax.all_to_all(
-        value, "row", split_axis=0, concat_axis=0, axis_index_groups=groups, tiled=True
+        value, "row", split_axis=0, concat_axis=0, axis_index_groups=LINES, tiled=True
     )
 
 
@@ -402,9 +415,9 @@
     other, gram, diag, eigvecs, reflectors = call(
         first_kernel,
         (
-            jax.ShapeDtypeStruct((CHIPS + 1, CHUNK, WIDTH), BF),
-            jax.ShapeDtypeStruct((CHIPS + 1, SHARE, WIDTH), BF),
-            jax.ShapeDtypeStruct((PANELS, WIDTH), F32),
+            pltpu.VMEM((CHIPS + 1, CHUNK, WIDTH), BF),
+            pltpu.VMEM((CHIPS + 1, SHARE, WIDTH), BF),
+            pltpu.VMEM((PANELS, WIDTH), F32),
             pltpu.VMEM(eigvecs.shape, BF),
             pltpu.VMEM(reflectors.shape, BF),
         ),
@@ -436,12 +449,12 @@
     )
     lot = jax.ShapeDtypeStruct((SIDE, CHUNK, WIDTH), BF)
     lots = jax.ShapeDtypeStruct((SIDE, SIDE * CHUNK, WIDTH), BF)
-    for groups in (WIDE, NARROW):
-        parts = exchanged(payload.reshape(SIDE, -1, WIDTH), groups)
-        payload = call(sum_kernel, lot, [VMEM], VMEM, 2**20, 2 * 2**20)(parts)
-    gathered = exchanged(payload, NARROW)
-    gathered = call(spread_kernel, lots, [VMEM], VMEM, 2**20, 2 * 2**20)(gathered)
-    mine = exchanged(gathered, WIDE).reshape(CHIPS, CHUNK, WIDTH)
+    parts = exchanged(payload.reshape(SIDE, -1, WIDTH))
+    sums = call(sum_kernel, lot, [VMEM], VMEM, 2**20, 2 * 2**20)(parts)
+    for pairs, shape in zip(SWAPS, (lot, lots)):
+        theirs = swapped(sums, pairs)
+        sums = call(add_kernel, shape, [VMEM] * 2, VMEM, 2**20, 2 * 2**20)(sums, theirs)
+    mine = exchanged(sums).reshape(CHIPS, CHUNK, WIDTH)
     theirs = swapped(mine[:, PROJ:MORE, :])
     scaled, dev = call(
         solve_kernel,

time: 86.6 us -> 79.8 us (0.921)
  blocking collectives: 52.4 us -> 32.6 us
  waiting for transfers between devices: 3.17 us -> 14.2 us
  starting transfers between devices: 7.38 us -> 11.8 us
  Pallas kernels: 22.4 us -> 20 us
    all_to_all x4 -> x2, blocking collectives: 52.4 us -> 32.6 us  [exchanged(): lax.all_to_all(value, 'row', split_axis=0, concat_axis=0, axis_index_grou...]
    ppermute x3 -> x5, waiting for transfers between devices: 3.17 us -> 14.2 us  [swapped(): return lax.ppermute(value, 'row', pairs)]
    ppermute x3 -> x5, starting transfers between devices: 7.38 us -> 11.8 us  [swapped(): return lax.ppermute(value, 'row', pairs)]
    pallas_call x4, Pallas kernels: 9.42 us -> 7.02 us  [the longest x1 6.56 us: steps(): call(first_kernel, (pltpu.VMEM((CHIPS + 1, CHUNK, WIDTH), BF), pltpu.VMEM...]
  transfers between devices with their start and end apart: 3 -> 5, of which waited for: 2 -> 4; matrix products, arithmetic and copies ran while one was open for 0% -> 0% of each run, Pallas kernels for 6% -> 6%
where the time goes in v6:
time: 79.8 us; the launch traced here: 79.6 us
  blocking collectives  32.6 us (41%)
  Pallas kernels  20 us (25%)
  waiting for transfers between devices  14.2 us (18%)
  starting transfers between devices  11.8 us (15%)
  between operations  0.85 us (1%)
    all_to_all x2, blocking collectives, exchanged(): lax.all_to_all(value, 'row', split_axis=0, concat_axis=0, axis_index_grou...  32.6 us
    ppermute x5, waiting for transfers between devices, swapped(): return lax.ppermute(value, 'row', pairs)  14.2 us
    ppermute x5, starting transfers between devices, swapped(): return lax.ppermute(value, 'row', pairs)  11.8 us
    pallas_call x2, Pallas kernels, update(): call(functools.partial(update_kernel, flip), out_shape, in_specs, out_spe...  6.71 us
    pallas_call x1, Pallas kernels, steps(): call(first_kernel, (pltpu.VMEM((CHIPS + 1, CHUNK, WIDTH), BF), pltpu.VMEM...  6.56 us
    pallas_call x1, Pallas kernels, steps(): call(solve_kernel, (jax.ShapeDtypeStruct((CHIPS, PROJ + TILE, WIDTH), BF)...  4.01 us
    pallas_call x1, Pallas kernels, steps(): call(own_kernel, (jax.ShapeDtypeStruct((CHIPS, PROJ, WIDTH), BF), jax.Sha...  1.85 us
  transfers between devices with their start and end apart: 5, of which 4 were waited for; matrix products, arithmetic and copies ran while one was open for 0% of the time, Pallas kernels for 6%

profile of v6, /device:TPU:1, one launch (start us, length us, event | category | flops | bytes accessed | tf_op | source)
XLA Modules:
  0.0 79.6 jit_solution(6159052749467922008)
XLA Ops:
  0.6 6.6 %shard_map.50 = (bf16[17,400,128]{2,1,0:T(8,128)(2,1)S(1)}, bf16[17,128,128]{2,1,0:T(8,128)(2,1)S(1)}, f32[8,128]{1,0:T(8,128)S(1)}, bf16[1536,1024]{1,0:T(8,128)(2,1)S(1)}, bf16[8,1536,128]{2,1,0:T(8,128)(2,1)S(1)}) custom-call(bf16[1536,1024]{1,0:T(8,128)(2,1)} %x_hbm.1, bf16[8,1536,128]{2,1,0:T(8,128)(2,1)} %v_hbm.1), custom_call_target="tpu_custom_call" | custom-call | flops 3221225472 | bytes 8388608 | tf_op jit(solution)/shard_map/pallas_call | solution.py:415
  7.2 1.4 %collective-permute-start = (bf16[17,400,128]{2,1,0:T(8,128)(2,1)S(1)}, bf16[17,400,128]{2,1,0:T(8,128)(2,1)S(1)}, u32[]{:S(2)}, u32[]{:S(2)}) collective-permute-start(bf16[17,400,128]{2,1,0:T(8,128)(2,1)S(1)} %get-tuple-element.19), channel_id=1, source_target_pairs={{4,0},{0,4},{12,8},{8,12},{20,16},{16,20},{28,24},{24,28},{36,32},... | collective-permute-start | bytes 5222408 | tf_op jit(solution)/shard_map/ppermute | solution.py:401
  8.6 1.9 %shard_map.51 = (bf16[16,256,128]{2,1,0:T(8,128)(2,1)S(1)}, f32[1,512]{1,0:T(1,128)S(1)}) custom-call(bf16[1536,1024]{1,0:T(8,128)(2,1)S(1)} %get-tuple-element.13.x_ref, bf16[8,1536,128]{2,1,0:T(8,128)(2,1)S(1)} %get-tuple-element.14.v_ref), custom_call_target="tpu_custom_call" | custom-call | flops 1610612736 | bytes 6291456 | tf_op jit(solution)/shard_map/pallas_call | solution.py:436
  10.5 1.4 %collective-permute-done.other_ref = bf16[17,400,128]{2,1,0:T(8,128)(2,1)S(1)} collective-permute-done((bf16[17,400,128]{2,1,0:T(8,128)(2,1)S(1)}, bf16[17,400,128]{2,1,0:T(8,128)(2,1)S(1)}, u32[]{:S(2)}, u32[]{:S(2)}) %collective-permute-start) | collective-permute-done | bytes 1740832 | tf_op jit(solution)/shard_map/ppermute | solution.py:401
  11.9 0.4 shard_map.52
  12.4 16.8 %all_to_all.10.parts_ref = bf16[4,1600,128]{2,1,0:T(8,128)(2,1)S(1)} all-to-all(bf16[4,1600,128]{2,1,0:T(8,128)(2,1)S(1)} %bitcast.5), channel_id=1, replica_groups={{0,8,16,24},{32,40,48,56},{64,72,80,88},{96,104,112,120},{4,36,68,100},..., dimensions={0} | all-to-all | bytes 3276800 | tf_op jit(solution)/shard_map/all_to_all | solution.py:405
  29.2 0.2 shard_map.53.mine_ref
  29.4 1.7 %collective-permute-start.1 = (bf16[4,400,128]{2,1,0:T(8,128)(2,1)S(1)}, bf16[4,400,128]{2,1,0:T(8,128)(2,1)S(1)}, u32[]{:S(2)}, u32[]{:S(2)}) collective-permute-start(bf16[4,400,128]{2,1,0:T(8,128)(2,1)S(1)} %shard_map.53.mine_ref), channel_id=1, source_target_pairs={{4,12},{12,4},{20,28},{28,20},{36,44},{44,36},{52,60},{60,52},{68,... | collective-permute-start | bytes 1228808 | tf_op jit(solution)/shard_map/ppermute | solution.py:401
  31.1 5.6 %collective-permute-done.1.theirs_ref = bf16[4,400,128]{2,1,0:T(8,128)(2,1)S(1)} collective-permute-done((bf16[4,400,128]{2,1,0:T(8,128)(2,1)S(1)}, bf16[4,400,128]{2,1,0:T(8,128)(2,1)S(1)}, u32[]{:S(2)}, u32[]{:S(2)}) %collective-permute-start.1) | collective-permute-done | bytes 409632 | tf_op jit(solution)/shard_map/ppermute | solution.py:401
  36.8 0.1 shard_map.54.mine_ref
  36.9 3.6 %collective-permute-start.2 = (bf16[4,400,128]{2,1,0:T(8,128)(2,1)S(1)}, bf16[4,400,128]{2,1,0:T(8,128)(2,1)S(1)}, u32[]{:S(2)}, u32[]{:S(2)}) collective-permute-start(bf16[4,400,128]{2,1,0:T(8,128)(2,1)S(1)} %shard_map.54.mine_ref), channel_id=1, source_target_pairs={{4,28},{12,20},{20,12},{28,4},{36,60},{44,52},{52,44},{60,36},{68,... | collective-permute-start | bytes 1228808 | tf_op jit(solution)/shard_map/ppermute | solution.py:401
  40.5 5.6 %collective-permute-done.2.theirs_ref = bf16[4,400,128]{2,1,0:T(8,128)(2,1)S(1)} collective-permute-done((bf16[4,400,128]{2,1,0:T(8,128)(2,1)S(1)}, bf16[4,400,128]{2,1,0:T(8,128)(2,1)S(1)}, u32[]{:S(2)}, u32[]{:S(2)}) %collective-permute-start.2) | collective-permute-done | bytes 409632 | tf_op jit(solution)/shard_map/ppermute | solution.py:401
  46.2 0.1 shard_map.55
  46.3 0.0 copy-start
  46.3 15.8 %all_to_all.11 = bf16[4,1600,128]{2,1,0:T(8,128)(2,1)S(1)} all-to-all(bf16[4,1600,128]{2,1,0:T(8,128)(2,1)S(1)} %shard_map.55), channel_id=1, replica_groups={{0,8,16,24},{32,40,48,56},{64,72,80,88},{96,104,112,120},{4,36,68,100},..., dimensions={0} | all-to-all | bytes 3276800 | tf_op jit(solution)/shard_map/all_to_all | solution.py:405
  62.1 4.4 %collective-permute-start.3 = (bf16[16,128,128]{2,1,0:T(8,128)(2,1)S(1)}, bf16[16,128,128]{2,1,0:T(8,128)(2,1)S(1)}, u32[]{:S(2)}, u32[]{:S(2)}) collective-permute-start(bf16[16,128,128]{2,1,0:T(8,128)(2,1)S(1)} %slice.4), channel_id=1, source_target_pairs={{4,0},{0,4},{12,8},{8,12},{20,16},{16,20},{28,24},{24,28},{36,32},... | collective-permute-start | bytes 1572872 | tf_op jit(solution)/shard_map/ppermute | solution.py:401
  66.5 1.5 %collective-permute-done.3.theirs_ref = bf16[16,128,128]{2,1,0:T(8,128)(2,1)S(1)} collective-permute-done((bf16[16,128,128]{2,1,0:T(8,128)(2,1)S(1)}, bf16[16,128,128]{2,1,0:T(8,128)(2,1)S(1)}, u32[]{:S(2)}, u32[]{:S(2)}) %collective-permute-start.3) | collective-permute-done | bytes 524320 | tf_op jit(solution)/shard_map/ppermute | solution.py:401
  68.0 0.0 copy-done
  68.0 4.0 %shard_map.56 = (bf16[16,272,128]{2,1,0:T(8,128)(2,1)S(1)}, f32[1,512]{1,0:T(1,128)S(1)}) custom-call(bf16[16,400,128]{2,1,0:T(8,128)(2,1)S(1)} %bitcast.4, bf16[16,128,128]{2,1,0:T(8,128)(2,1)S(1)} %collective-permute-done.3.theirs_ref, f32[8,128,128]{2,1,0:T(8,128)S(1)} %copy-done), custom_call_target="tpu_custom_call" | custom-call | flops 268435456 | bytes 4194304 | tf_op jit(solution)/shard_map/pallas_call | solution.py:459
  72.1 0.6 collective-permute-start.4
  72.7 3.0 %shard_map.57.refs_0_ = bf16[1536,1024]{1,0:T(8,128)(2,1)} custom-call(bf16[1536,1024]{1,0:T(8,128)(2,1)S(1)} %get-tuple-element.13.x_ref, bf16[8,1536,128]{2,1,0:T(8,128)(2,1)S(1)} %get-tuple-element.14.v_ref, bf16[16,272,128]{2,1,0:T(8,128)(2,1)S(1)} %get-tuple-element.20.s_ref), custom_call_target="tpu_custom_call" | custom-call | flops 1610612736 | bytes 6291456 | tf_op jit(solution)/shard_map/pallas_call | solution.py:382
  75.7 0.0 collective-permute-done.4.s_ref
  75.7 3.7 %shard_map.58 = (bf16[1536,1024]{1,0:T(8,128)(2,1)}, f32[1,1024]{1,0:T(1,128)}) custom-call(bf16[1536,1024]{1,0:T(8,128)(2,1)S(1)} %get-tuple-element.13.x_ref, bf16[8,1536,128]{2,1,0:T(8,128)(2,1)S(1)} %get-tuple-element.14.v_ref, bf16[16,272,128]{2,1,0:T(8,128)(2,1)S(1)} %collective-permute-done.4.s_ref, ...), custom_call_target="tpu_custom_call", output_to_operand_aliasing={{0}: (3, {})} | custom-call | flops 1610612736 | bytes 6291456 | tf_op jit(solution)/shard_map/pallas_call | solution.py:382
  (1 shorter events, 0.0 us)
Async XLA Ops:
  7.2 4.7 %collective-permute-start = (bf16[17,400,128]{2,1,0:T(8,128)(2,1)S(1)}, bf16[17,400,128]{2,1,0:T(8,128)(2,1)S(1)}, u32[]{:S(2)}, u32[]{:S(2)}) collective-permute-start(bf16[17,400,128]{2,1,0:T(8,128)(2,1)S(1)} %get-tuple-element.19), channel_id=1, source_target_pairs={{4,0},{0,4},{12,8},{8,12},{20,16},{16,20},{28,24},{24,28},{36,32},... | collective-permute-start | bytes 5222408 | tf_op jit(solution)/shard_map/ppermute | solution.py:401
  29.4 7.4 %collective-permute-start.1 = (bf16[4,400,128]{2,1,0:T(8,128)(2,1)S(1)}, bf16[4,400,128]{2,1,0:T(8,128)(2,1)S(1)}, u32[]{:S(2)}, u32[]{:S(2)}) collective-permute-start(bf16[4,400,128]{2,1,0:T(8,128)(2,1)S(1)} %shard_map.53.mine_ref), channel_id=1, source_target_pairs={{4,12},{12,4},{20,28},{28,20},{36,44},{44,36},{52,60},{60,52},{68,... | collective-permute-start | bytes 1228808 | tf_op jit(solution)/shard_map/ppermute | solution.py:401
  36.9 9.3 %collective-permute-start.2 = (bf16[4,400,128]{2,1,0:T(8,128)(2,1)S(1)}, bf16[4,400,128]{2,1,0:T(8,128)(2,1)S(1)}, u32[]{:S(2)}, u32[]{:S(2)}) collective-permute-start(bf16[4,400,128]{2,1,0:T(8,128)(2,1)S(1)} %shard_map.54.mine_ref), channel_id=1, source_target_pairs={{4,28},{12,20},{20,12},{28,4},{36,60},{44,52},{52,44},{60,36},{68,... | collective-permute-start | bytes 1228808 | tf_op jit(solution)/shard_map/ppermute | solution.py:401
  46.3 21.7 %copy-start = (f32[8,128,128]{2,1,0:T(8,128)S(1)}, f32[8,128,128]{2,1,0:T(8,128)}, u32[]{:S(2)}) copy-start(f32[8,128,128]{2,1,0:T(8,128)} %t_ref.1) | copy-start | bytes 1572868
  62.1 5.9 %collective-permute-start.3 = (bf16[16,128,128]{2,1,0:T(8,128)(2,1)S(1)}, bf16[16,128,128]{2,1,0:T(8,128)(2,1)S(1)}, u32[]{:S(2)}, u32[]{:S(2)}) collective-permute-start(bf16[16,128,128]{2,1,0:T(8,128)(2,1)S(1)} %slice.4), channel_id=1, source_target_pairs={{4,0},{0,4},{12,8},{8,12},{20,16},{16,20},{28,24},{24,28},{36,32},... | collective-permute-start | bytes 1572872 | tf_op jit(solution)/shard_map/ppermute | solution.py:401
  72.1 3.7 %collective-permute-start.4 = (bf16[16,272,128]{2,1,0:T(8,128)(2,1)S(1)}, bf16[16,272,128]{2,1,0:T(8,128)(2,1)S(1)}, u32[]{:S(2)}, u32[]{:S(2)}) collective-permute-start(bf16[16,272,128]{2,1,0:T(8,128)(2,1)S(1)} %get-tuple-element.20.s_ref), channel_id=1, source_target_pairs={{4,0},{0,4},{12,8},{8,12},{20,16},{16,20},{28,24},{24,28},{36,32},... | collective-permute-start | bytes 3342344 | tf_op jit(solution)/shard_map/ppermute | solution.py:401
